TPU v7x, 768 devices: a whole 4x8x12 slice. The times are simulated.
768 devices in a mesh: pipe: 12 (over z), dp: 16 (over x, y_hi), tensor: 4 (over y_lo, core).
Axes of the slice: x: 4, y: 8 (y_hi: 4, y_lo: 2; y = y_hi * 2 + y_lo), z: 12, core: 2. Of those that a mesh axis runs over, the one named last changes fastest.
Arguments:
- saved_inputs: bfloat16 [3, 2, 12, 2048, 4096], P(None, None, 'pipe', 'dp', 'tensor'), may hold values from -6 to 6
- proj_in: bfloat16 [2, 12, 512, 4096], P(None, 'pipe', None, 'tensor'), may hold values from -0.09375 to 0.09375
- proj_out: bfloat16 [2, 12, 512, 4096], P(None, 'pipe', None, 'tensor'), may hold values from -0.25 to 0.25
- norm_gain: float32 [2, 12, 4096], P(None, 'pipe', 'tensor'), may hold values from 0.1 to 1.9
- arriving: bfloat16 [2, 12, 2048, 4096], P(None, 'pipe', 'dp', 'tensor'), may hold values from -6 to 6
- logp_grad: bfloat16 [2, 2048, 4096], P(None, 'dp', 'tensor'), may hold values from -6 to 6
- rewards: float32 [2, 16, 4], P(None, 'dp'), may hold values from -4 to 4
- seq_lengths: int32 [2, 16, 4], P(None, 'dp'), may hold values from 1 to 64, 128 in all within a row
- group_ids: int32 [2, 16, 4], P(None, 'dp'), may hold values from 0 to 15
Outputs:
- grad_in: float32 [2, 12, 512, 4096], P(None, 'pipe', 'dp', 'tensor')
- grad_out: float32 [2, 12, 512, 4096], P(None, 'pipe', 'dp', 'tensor')
- leaving: bfloat16 [2, 12, 2048, 4096], P(None, 'pipe', 'dp', 'tensor')
Inputs may be any that keep to these rules, and one draw needn't show every extreme that they name: `seq_lengths`: the 4 lengths of one microbatch on one replica sum to 128. `group_ids`: groups take sequences from several replicas and microbatches.
All inputs are finite; a program needn't handle non-finite values.
Results may differ from a plain program's by a relative error of at most 0.023.
Values may be sent and summed in bfloat16 or wider, within the bound.
A program may use at most 64 MiB of HBM per device.

v0:
```python
import jax
import jax.numpy as jnp
from jax import lax
from jax.sharding import PartitionSpec as P

D = 4096


EPS = 1e-05


def from_everyone(x, axis):
    copies = jnp.broadcast_to(x, (lax.axis_size(axis), *x.shape))
    return lax.all_to_all(copies, axis, split_axis=0, concat_axis=0, tiled=True)


def of_everyone(x, axis):
    everything = from_everyone(x, axis)
    return jnp.sum(everything.astype(jnp.float32), axis=0)


def of_everyone_2(x, axis):
    return from_everyone(x, axis).sum(axis=0)


def together(arrays, axis):
    ends = [0]
    for a in arrays:
        ends.append(ends[-1] + a.size)
    so_far = of_everyone_2(jnp.concatenate([a.ravel() for a in arrays]), axis)
    return tuple((so_far[b:e].reshape(a.shape) for a, b, e in zip(arrays, ends, ends[1:])))


def shifted(x, axis, by):
    count = lax.axis_size(axis)
    return lax.ppermute(x, axis, [(i, (i + by) % count) for i in range(count)])


def sent_together(arrays, axis, dim, along):
    widths = [a.shape[along] for a in arrays]
    both = jnp.concatenate(arrays, axis=along)
    whole = lax.psum_scatter(both, axis, scatter_dimension=dim, tiled=True)
    return tuple(jnp.split(whole, [sum(widths[:k]) for k in range(1, len(widths))], axis=along))


def silu_slope(values):
    sigma = jax.nn.sigmoid(values)
    return sigma * (1.0 + values * (1.0 - sigma))


def block_back(inputs, arrive, weight_in, weight_out, gain_rows, inv_rms):
    inputs_f = inputs.astype(jnp.float32)
    gained = (inputs_f * gain_rows[:, None, :]).astype(jnp.bfloat16)
    part_pre = jnp.einsum("vrd,vkd->vrk", gained, weight_in, preferred_element_type=jnp.float32)
    part_back = jnp.einsum("vrd,vkd->vrk", arrive, weight_out, preferred_element_type=jnp.float32)
    pre_sum, back_sum = (
        of_everyone(part_pre.astype(jnp.bfloat16), "tensor").astype(jnp.float32),
        of_everyone(part_back.astype(jnp.bfloat16), "tensor").astype(jnp.float32),
    )
    scaled = inv_rms[..., None]
    pre_act = scaled * pre_sum
    hidden = jax.nn.silu(pre_act).astype(jnp.bfloat16)
    grad_pre = back_sum * silu_slope(pre_act)
    grad_scaled = (scaled * grad_pre).astype(jnp.bfloat16)
    term_in = jnp.einsum("vrk,vrd->vkd", grad_scaled, gained, preferred_element_type=jnp.float32)
    term_out = jnp.einsum("vrk,vrd->vkd", hidden, arrive, preferred_element_type=jnp.float32)
    grad_gained = jnp.einsum(
        "vrk,vkd->vrd", grad_scaled, weight_in, preferred_element_type=jnp.float32
    )
    radial_sum = jnp.sum(grad_pre * pre_sum, axis=-1)
    out_cot = (
        arrive.astype(jnp.float32)
        + gain_rows[:, None, :] * grad_gained
        - inputs_f * (inv_rms**3 * radial_sum / D)[..., None]
    )
    return (out_cot.astype(jnp.bfloat16), term_in, term_out)


def shards(
    saved_inputs, proj_in, proj_out, norm_gain, arriving, logp_grad, rewards, seq_lengths, group_ids
):
    sections = lax.axis_size("pipe")
    section = lax.axis_index("pipe")
    replicas = lax.axis_size("dp")
    saved = saved_inputs[:, :, 0]
    weights_in = proj_in[:, 0]
    weights_out = proj_out[:, 0]
    gains = norm_gain[:, 0]
    current = arriving[:, 0]
    step_count = saved.shape[0]
    local_rows = saved.shape[2]
    new_count = logp_grad.shape[0]
    seq_count = rewards.shape[2]
    group_count = new_count * replicas * seq_count // 8
    saved_f = saved.astype(jnp.float32)
    squares = jnp.sum(saved_f * saved_f, axis=-1)
    totals = of_everyone_2(squares, "tensor")
    inv_rms_all = 1.0 / jnp.sqrt(totals / D + EPS)
    groups = jnp.arange(group_count, dtype=jnp.int32)
    member = (group_ids[..., None] == groups).astype(jnp.float32)
    sums = jnp.sum(member * rewards[..., None], axis=(0, 1, 2))
    counts = jnp.sum(member, axis=(0, 1, 2))
    sums, counts = together((sums, counts), "dp")
    means = sums / jnp.maximum(counts, 1.0)
    advantage = rewards - jnp.sum(member * means, axis=-1)
    ends = jnp.cumsum(seq_lengths, axis=-1)
    position = jnp.arange(local_rows, dtype=jnp.int32)
    segment = jnp.sum((position[:, None] >= ends[..., None, :]).astype(jnp.int32), axis=-1)
    pick = (segment[..., None] == jnp.arange(seq_count, dtype=jnp.int32)).astype(jnp.float32)
    token_weight = jnp.sum(pick * advantage[..., None, :], axis=-1)[:, 0]
    entering = (-token_weight[..., None] * logp_grad.astype(jnp.float32)).astype(jnp.bfloat16)

    def run_blocks(first, last, arrive, step_index):
        return block_back(
            saved[step_index, first:last],
            arrive,
            weights_in,
            weights_out,
            gains,
            inv_rms_all[step_index, first:last],
        )

    is_top = section == sections - 1
    acc_in = jnp.zeros((2,) + weights_in.shape[1:], jnp.float32)
    acc_out = jnp.zeros((2,) + weights_in.shape[1:], jnp.float32)
    for step_index in range(step_count - 1):
        moved, add_in, add_out = run_blocks(0, 2, current, step_index)
        acc_in = acc_in + add_in
        acc_out = acc_out + add_out
        received = shifted(moved, "pipe", -1)
        from_upper = received[1]
        from_lower = received[0]
        upper_next = jnp.where(is_top, entering[step_index], from_upper)
        lower_next = jnp.where(is_top, from_upper, from_lower)
        current = jnp.stack([lower_next, upper_next])
    final_index = step_count - 1
    leaving, add_in, add_out = run_blocks(0, 2, current, final_index)
    summed_in, summed_out = tuple(
        (
            part.astype(jnp.float32)
            for part in sent_together(
                ((acc_in + add_in).astype(jnp.bfloat16), (acc_out + add_out).astype(jnp.bfloat16)),
                "dp",
                1,
                0,
            )
        )
    )
    scale = 1.0 / (replicas * local_rows)
    return ((summed_in * scale)[:, None], (summed_out * scale)[:, None], leaving[:, None])


def solution(mesh):
    return jax.shard_map(
        shards,
        mesh=mesh,
        in_specs=(
            P(None, None, "pipe", "dp", "tensor"),
            P(None, "pipe", None, "tensor"),
            P(None, "pipe", None, "tensor"),
            P(None, "pipe", "tensor"),
            P(None, "pipe", "dp", "tensor"),
            P(None, "dp", "tensor"),
            P(None, "dp", None),
            P(None, "dp", None),
            P(None, "dp", None),
        ),
        out_specs=(
            P(None, "pipe", "dp", "tensor"),
            P(None, "pipe", "dp", "tensor"),
            P(None, "pipe", "dp", "tensor"),
        ),
        check_vma=False,
    )
```

profile of v0, /device:TPU:2, one launch (start us, length us, event | category | flops | bytes accessed | tf_op | source)
XLA Modules:
  0.0 297.8 jit_solution(14250904702772432956)
XLA Ops:
  8.8 12.8 %all-to-all-start.3 = ((f32[16,1,32]{2,1,0:T(1,128)}), f32[16,1,32]{2,1,0:T(1,128)S(1)}, u32[]{:S(2)}, u32[]{:S(2)}) async-start(f32[16,1,32]{2,1,0:T(1,128)} %broadcast_in_dim.47), calls=%async_computation.3 | async-start | bytes 16384 | tf_op jit(solution)/shard_map/all_to_all | solution.py:14
  24.1 6.1 %all-to-all-done.3 = f32[16,1,32]{2,1,0:T(1,128)S(1)} async-done(((f32[16,1,32]{2,1,0:T(1,128)}), f32[16,1,32]{2,1,0:T(1,128)S(1)}, u32[]{:S(2)}, u32[]{:S(2)}) %all-to-all-start.3) | async-done | bytes 2080 | tf_op jit(solution)/shard_map/all_to_all | solution.py:14
  30.8 3.3 %all-to-all-start = ((f32[4,3,2,128]{3,2,1,0:T(2,128)}), f32[4,3,2,128]{3,2,1,0:T(2,128)S(1)}, u32[]{:S(2)}, u32[]{:S(2)}) async-start(f32[4,3,2,128]{3,2,1,0:T(2,128)} %broadcast_in_dim.44), calls=%async_computation | async-start | bytes 24576 | tf_op jit(solution)/shard_map/all_to_all | solution.py:14
  34.1 1.9 fusion.45
  36.0 1.9 all-to-all-done
  39.0 3.5 %all-to-all-start.2 = ((bf16[4,2,128,512]{3,2,1,0:T(8,128)(2,1)}), bf16[4,2,128,512]{3,2,1,0:T(8,128)(2,1)S(1)}, u32[]{:S(2)}, u32[]{:S(2)}) async-start(bf16[4,2,128,512]{3,2,1,0:T(8,128)(2,1)} %broadcast_in_dim.46), calls=%async_computation.2 | async-start | bytes 2097152 | tf_op jit(solution)/shard_map/all_to_all | solution.py:14
  42.5 2.6 fusion.36
  45.1 11.8 %all-to-all-done.2 = bf16[4,2,128,512]{3,2,1,0:T(8,128)(2,1)S(1)} async-done(((bf16[4,2,128,512]{3,2,1,0:T(8,128)(2,1)}), bf16[4,2,128,512]{3,2,1,0:T(8,128)(2,1)S(1)}, u32[]{:S(2)}, u32[]{:S(2)}) %all-to-all-start.2) | async-done | bytes 1048608 | tf_op jit(solution)/shard_map/all_to_all | solution.py:14
  58.0 4.4 %all-to-all-start.1 = ((bf16[4,2,128,512]{3,2,1,0:T(8,128)(2,1)}), bf16[4,2,128,512]{3,2,1,0:T(8,128)(2,1)}, u32[]{:S(2)}, u32[]{:S(2)}) async-start(bf16[4,2,128,512]{3,2,1,0:T(8,128)(2,1)} %broadcast_in_dim.45), calls=%async_computation.1 | async-start | bytes 2097152 | tf_op jit(solution)/shard_map/all_to_all | solution.py:14
  66.3 10.6 %all-to-all-done.1 = bf16[4,2,128,512]{3,2,1,0:T(8,128)(2,1)} async-done(((bf16[4,2,128,512]{3,2,1,0:T(8,128)(2,1)}), bf16[4,2,128,512]{3,2,1,0:T(8,128)(2,1)}, u32[]{:S(2)}, u32[]{:S(2)}) %all-to-all-start.1) | async-done | bytes 1048608 | tf_op jit(solution)/shard_map/all_to_all | solution.py:14
  78.0 4.4 %all-to-all-start.5 = ((bf16[4,2,128,512]{3,2,1,0:T(8,128)(2,1)}), bf16[4,2,128,512]{3,2,1,0:T(8,128)(2,1)}, u32[]{:S(2)}, u32[]{:S(2)}) async-start(bf16[4,2,128,512]{3,2,1,0:T(8,128)(2,1)} %broadcast_in_dim.49), calls=%async_computation.5 | async-start | bytes 2097152 | tf_op jit(solution)/shard_map/all_to_all | solution.py:14
  84.3 1.9 fusion.33
  86.2 12.0 %collective-permute-start = (bf16[2,128,1024]{2,1,0:T(8,128)(2,1)S(1)}, bf16[2,128,1024]{2,1,0:T(8,128)(2,1)S(1)}, u32[]{:S(2)}, u32[]{:S(2)}) collective-permute-start(bf16[2,128,1024]{2,1,0:T(8,128)(2,1)S(1)} %fusion.33), channel_id=1, source_target_pairs={{0,704},{64,0},{128,64},{192,128},{256,192},{320,256},{384,320},{4... | collective-permute-start | bytes 1572872 | tf_op jit(solution)/shard_map/ppermute | solution.py:36
  98.5 11.5 %collective-permute-done = bf16[2,128,1024]{2,1,0:T(8,128)(2,1)S(1)} collective-permute-done((bf16[2,128,1024]{2,1,0:T(8,128)(2,1)S(1)}, bf16[2,128,1024]{2,1,0:T(8,128)(2,1)S(1)}, u32[]{:S(2)}, u32[]{:S(2)}) %collective-permute-start) | collective-permute-done | bytes 524320 | tf_op jit(solution)/shard_map/ppermute | solution.py:36
  112.0 4.3 %all-to-all-start.4 = ((bf16[4,2,128,512]{3,2,1,0:T(8,128)(2,1)}), bf16[4,2,128,512]{3,2,1,0:T(8,128)(2,1)}, u32[]{:S(2)}, u32[]{:S(2)}) async-start(bf16[4,2,128,512]{3,2,1,0:T(8,128)(2,1)} %broadcast_in_dim.48), calls=%async_computation.4 | async-start | bytes 2097152 | tf_op jit(solution)/shard_map/all_to_all | solution.py:14
  116.3 1.9 fusion.51
  118.2 12.6 %all-to-all-done.4 = bf16[4,2,128,512]{3,2,1,0:T(8,128)(2,1)} async-done(((bf16[4,2,128,512]{3,2,1,0:T(8,128)(2,1)}), bf16[4,2,128,512]{3,2,1,0:T(8,128)(2,1)}, u32[]{:S(2)}, u32[]{:S(2)}) %all-to-all-start.4) | async-done | bytes 1048608 | tf_op jit(solution)/shard_map/all_to_all | solution.py:14
  131.9 4.3 %all-to-all-start.7 = ((bf16[4,2,128,512]{3,2,1,0:T(8,128)(2,1)}), bf16[4,2,128,512]{3,2,1,0:T(8,128)(2,1)}, u32[]{:S(2)}, u32[]{:S(2)}) async-start(bf16[4,2,128,512]{3,2,1,0:T(8,128)(2,1)} %broadcast_in_dim.51), calls=%async_computation.7 | async-start | bytes 2097152 | tf_op jit(solution)/shard_map/all_to_all | solution.py:14
  139.6 2.7 fusion.57
  142.3 5.6 %collective-permute-start.1 = (bf16[2,128,1024]{2,1,0:T(8,128)(2,1)}, bf16[2,128,1024]{2,1,0:T(8,128)(2,1)}, u32[]{:S(2)}, u32[]{:S(2)}) collective-permute-start(bf16[2,128,1024]{2,1,0:T(8,128)(2,1)} %fusion.57), channel_id=1, source_target_pairs={{0,704},{64,0},{128,64},{192,128},{256,192},{320,256},{384,320},{4... | collective-permute-start | bytes 1572872 | tf_op jit(solution)/shard_map/ppermute | solution.py:36
  147.9 2.7 all-to-all-done.7
  152.1 4.1 %fusion.74 = f32[2,512,1024]{2,1,0:T(8,128)} fusion(f32[2,1024]{1,0:T(2,128)S(1)} %bitcast.136, bf16[3,2,1,128,1024]{4,3,1,2,0:T(8,128)(2,1)} %bitcast.127, f32[2,128]{1,0:T(2,128)S(1)} %get-tuple-element.22, f32[2,128,512]{2,1,0:T(8,128)} %copy-done.4, f32[2,128,512]{2,1,0:T(8,128)S(1)} %convert_reduce_fusion.4), kind=kOutput, calls=%fused_computation.79 | convolution fusion | flops 270663680 | bytes 5776384 | tf_op jit(solution)/shard_map/vrk,vrd->vkd/dot_general | solution.py:65
  156.2 3.8 %collective-permute-done.1 = bf16[2,128,1024]{2,1,0:T(8,128)(2,1)} collective-permute-done((bf16[2,128,1024]{2,1,0:T(8,128)(2,1)}, bf16[2,128,1024]{2,1,0:T(8,128)(2,1)}, u32[]{:S(2)}, u32[]{:S(2)}) %collective-permute-start.1) | collective-permute-done | bytes 524320 | tf_op jit(solution)/shard_map/ppermute | solution.py:36
  163.0 4.3 %all-to-all-start.6 = ((bf16[4,2,128,512]{3,2,1,0:T(8,128)(2,1)}), bf16[4,2,128,512]{3,2,1,0:T(8,128)(2,1)}, u32[]{:S(2)}, u32[]{:S(2)}) async-start(bf16[4,2,128,512]{3,2,1,0:T(8,128)(2,1)} %broadcast_in_dim.50), calls=%async_computation.6 | async-start | bytes 2097152 | tf_op jit(solution)/shard_map/all_to_all | solution.py:14
  167.6 2.0 fusion.62
  170.6 4.0 %fusion.71 = f32[2,512,1024]{2,1,0:T(8,128)} fusion(f32[2,1024]{1,0:T(2,128)S(1)} %bitcast.137, bf16[3,2,1,128,1024]{4,3,1,2,0:T(8,128)(2,1)} %bitcast.128, f32[2,128]{1,0:T(2,128)S(1)} %get-tuple-element.21, f32[2,128,512]{2,1,0:T(8,128)S(1)} %copy-done.6, f32[2,128,512]{2,1,0:T(8,128)S(1)} %copy-done.2), kind=kOutput, calls=%fused_computation.78 | convolution fusion | flops 270663680 | bytes 5776384 | tf_op jit(solution)/shard_map/vrk,vrd->vkd/dot_general | solution.py:65
  174.5 2.2 add_convert_fusion
  176.8 5.0 %all-to-all-done.6 = bf16[4,2,128,512]{3,2,1,0:T(8,128)(2,1)} async-done(((bf16[4,2,128,512]{3,2,1,0:T(8,128)(2,1)}), bf16[4,2,128,512]{3,2,1,0:T(8,128)(2,1)}, u32[]{:S(2)}, u32[]{:S(2)}) %all-to-all-start.6) | async-done | bytes 1048608 | tf_op jit(solution)/shard_map/all_to_all | solution.py:14
  183.2 4.7 %add_convert_fusion.1 = bf16[2,512,1024]{2,1,0:T(8,128)(2,1)S(1)} fusion(f32[2,512,1024]{2,1,0:T(8,128)} %fusion.74, f32[2,512,1024]{2,1,0:T(8,128)} %fusion.71, f32[2,1024]{1,0:T(2,128)S(1)} %bitcast.138, bf16[3,2,1,128,1024]{4,3,1,2,0:T(8,128)(2,1)} %bitcast.129, f32[2,128]{1,0:T(2,128)S(1)} %get-tuple-element.20, ...), kind=kOutput, calls=%fused_computation.2 | convolution fusion | flops 273809408 | bytes 12067840 | tf_op jit(solution)/shard_map/vrk,vrd->vkd/dot_general | solution.py:65
  188.0 2.3 pad_maximum_fusion
  190.7 2.7 fusion.61
  193.4 95.7 %reduce-scatter.2.cloned.1.call-done = bf16[4,32,1024]{2,1,0:T(8,128)(2,1)} async-done(((bf16[4,512,1024]{2,1,0:T(8,128)(2,1)}), bf16[4,32,1024]{2,1,0:T(8,128)(2,1)}) %reduce-scatter.2.cloned.1.call-update) | async-done | bytes 262160 | tf_op jit(solution)/shard_map/reduce_scatter | solution.py:42
  (92 shorter events, 29.9 us)
Async XLA Ops:
  7.2 26.9 %copy-start = (bf16[2,1,512,1024]{3,2,1,0:T(8,128)(2,1)S(1)}, bf16[2,1,512,1024]{3,2,1,0:T(8,128)(2,1)}, u32[]{:S(2)}) copy-start(bf16[2,1,512,1024]{3,2,1,0:T(8,128)(2,1)} %param.10) | copy-start | bytes 6291460
  8.8 21.4 %all-to-all-start.3 = ((f32[16,1,32]{2,1,0:T(1,128)}), f32[16,1,32]{2,1,0:T(1,128)S(1)}, u32[]{:S(2)}, u32[]{:S(2)}) async-start(f32[16,1,32]{2,1,0:T(1,128)} %broadcast_in_dim.47), calls=%async_computation.3 | async-start | bytes 16384 | tf_op jit(solution)/shard_map/all_to_all | solution.py:14
  30.8 7.1 %all-to-all-start = ((f32[4,3,2,128]{3,2,1,0:T(2,128)}), f32[4,3,2,128]{3,2,1,0:T(2,128)S(1)}, u32[]{:S(2)}, u32[]{:S(2)}) async-start(f32[4,3,2,128]{3,2,1,0:T(2,128)} %broadcast_in_dim.44), calls=%async_computation | async-start | bytes 24576 | tf_op jit(solution)/shard_map/all_to_all | solution.py:14
  39.0 17.9 %all-to-all-start.2 = ((bf16[4,2,128,512]{3,2,1,0:T(8,128)(2,1)}), bf16[4,2,128,512]{3,2,1,0:T(8,128)(2,1)S(1)}, u32[]{:S(2)}, u32[]{:S(2)}) async-start(bf16[4,2,128,512]{3,2,1,0:T(8,128)(2,1)} %broadcast_in_dim.46), calls=%async_computation.2 | async-start | bytes 2097152 | tf_op jit(solution)/shard_map/all_to_all | solution.py:14
  45.1 17.4 %copy-start.22 = (s32[2,1,4]{2,1,0:T(1,128)S(1)}, s32[2,1,4]{2,1,0:T(1,128)}, u32[]{:S(2)}) copy-start(s32[2,1,4]{2,1,0:T(1,128)} %param.16) | copy-start | bytes 100
  56.9 7.7 %copy-start.7 = (bf16[4,2,128,512]{3,2,1,0:T(8,128)(2,1)}, bf16[4,2,128,512]{3,2,1,0:T(8,128)(2,1)S(1)}, u32[]{:S(2)}) copy-start(bf16[4,2,128,512]{3,2,1,0:T(8,128)(2,1)S(1)} %all-to-all-done.2) | copy-start | bytes 3145732
  58.0 6.7 %copy-start.21 = (s32[2,1,4]{2,1,0:T(1,128)S(1)}, s32[2,1,4]{2,1,0:T(1,128)}, u32[]{:S(2)}) copy-start(s32[2,1,4]{2,1,0:T(1,128)} %param.17) | copy-start | bytes 100
  58.0 18.9 %all-to-all-start.1 = ((bf16[4,2,128,512]{3,2,1,0:T(8,128)(2,1)}), bf16[4,2,128,512]{3,2,1,0:T(8,128)(2,1)}, u32[]{:S(2)}, u32[]{:S(2)}) async-start(bf16[4,2,128,512]{3,2,1,0:T(8,128)(2,1)} %broadcast_in_dim.45), calls=%async_computation.1 | async-start | bytes 2097152 | tf_op jit(solution)/shard_map/all_to_all | solution.py:14
  78.0 6.2 %copy-start.12 = (bf16[2,1,128,1024]{3,2,1,0:T(8,128)(2,1)S(1)}, bf16[2,1,128,1024]{3,2,1,0:T(8,128)(2,1)}, u32[]{:S(2)}) copy-start(bf16[2,1,128,1024]{3,2,1,0:T(8,128)(2,1)} %param.13) | copy-start | bytes 1572868
  78.0 32.9 %all-to-all-start.5 = ((bf16[4,2,128,512]{3,2,1,0:T(8,128)(2,1)}), bf16[4,2,128,512]{3,2,1,0:T(8,128)(2,1)}, u32[]{:S(2)}, u32[]{:S(2)}) async-start(bf16[4,2,128,512]{3,2,1,0:T(8,128)(2,1)} %broadcast_in_dim.49), calls=%async_computation.5 | async-start | bytes 2097152 | tf_op jit(solution)/shard_map/all_to_all | solution.py:14
  83.8 2.4 copy-start.4
  84.2 13.9 %copy-start.20 = (f32[2,1,4]{2,1,0:T(1,128)S(1)}, f32[2,1,4]{2,1,0:T(1,128)}, u32[]{:S(2)}) copy-start(f32[2,1,4]{2,1,0:T(1,128)} %param.15) | copy-start | bytes 100
  84.3 14.1 %copy-start.19 = (bf16[2,128,1024]{2,1,0:T(8,128)(2,1)S(1)}, bf16[2,128,1024]{2,1,0:T(8,128)(2,1)}, u32[]{:S(2)}) copy-start(bf16[2,128,1024]{2,1,0:T(8,128)(2,1)} %param.14) | copy-start | bytes 1572868
  86.2 23.8 %copy-start.10 = (bf16[2,1,512,1024]{3,2,1,0:T(8,128)(2,1)S(1)}, bf16[2,1,512,1024]{3,2,1,0:T(8,128)(2,1)}, u32[]{:S(2)}) copy-start(bf16[2,1,512,1024]{3,2,1,0:T(8,128)(2,1)} %param.11) | copy-start | bytes 6291460
  86.2 23.8 %collective-permute-start = (bf16[2,128,1024]{2,1,0:T(8,128)(2,1)S(1)}, bf16[2,128,1024]{2,1,0:T(8,128)(2,1)S(1)}, u32[]{:S(2)}, u32[]{:S(2)}) collective-permute-start(bf16[2,128,1024]{2,1,0:T(8,128)(2,1)S(1)} %fusion.33), channel_id=1, source_target_pairs={{0,704},{64,0},{128,64},{192,128},{256,192},{320,256},{384,320},{4... | collective-permute-start | bytes 1572872 | tf_op jit(solution)/shard_map/ppermute | solution.py:36
  98.5 11.5 %copy-start.8 = (bf16[2,128,1024]{2,1,0:T(8,128)(2,1)}, bf16[2,128,1024]{2,1,0:T(8,128)(2,1)S(1)}, u32[]{:S(2)}) copy-start(bf16[2,128,1024]{2,1,0:T(8,128)(2,1)S(1)} %multiply_convert_fusion) | copy-start | bytes 1572868
  110.0 29.6 %copy-start.13 = (bf16[1,128,1024]{2,1,0:T(8,128)(2,1)}, bf16[1,128,1024]{2,1,0:T(8,128)(2,1)S(1)}, u32[]{:S(2)}) copy-start(bf16[1,128,1024]{2,1,0:T(8,128)(2,1)S(1)} %get-tuple-element.17) | copy-start | bytes 786436
  112.0 18.8 %all-to-all-start.4 = ((bf16[4,2,128,512]{3,2,1,0:T(8,128)(2,1)}), bf16[4,2,128,512]{3,2,1,0:T(8,128)(2,1)}, u32[]{:S(2)}, u32[]{:S(2)}) async-start(bf16[4,2,128,512]{3,2,1,0:T(8,128)(2,1)} %broadcast_in_dim.48), calls=%async_computation.4 | async-start | bytes 2097152 | tf_op jit(solution)/shard_map/all_to_all | solution.py:14
  131.9 18.8 %all-to-all-start.7 = ((bf16[4,2,128,512]{3,2,1,0:T(8,128)(2,1)}), bf16[4,2,128,512]{3,2,1,0:T(8,128)(2,1)}, u32[]{:S(2)}, u32[]{:S(2)}) async-start(bf16[4,2,128,512]{3,2,1,0:T(8,128)(2,1)} %broadcast_in_dim.51), calls=%async_computation.7 | async-start | bytes 2097152 | tf_op jit(solution)/shard_map/all_to_all | solution.py:14
  137.6 4.7 %copy-start.1 = (f32[2,128,512]{2,1,0:T(8,128)}, f32[2,128,512]{2,1,0:T(8,128)S(1)}, u32[]{:S(2)}) copy-start(f32[2,128,512]{2,1,0:T(8,128)S(1)} %convert_reduce_fusion.2) | copy-start | bytes 1572868
  139.2 3.1 %copy-start.5 = (f32[2,128,512]{2,1,0:T(8,128)}, f32[2,128,512]{2,1,0:T(8,128)S(1)}, u32[]{:S(2)}) copy-start(f32[2,128,512]{2,1,0:T(8,128)S(1)} %convert_reduce_fusion.3) | copy-start | bytes 1572868
  142.3 17.7 %collective-permute-start.1 = (bf16[2,128,1024]{2,1,0:T(8,128)(2,1)}, bf16[2,128,1024]{2,1,0:T(8,128)(2,1)}, u32[]{:S(2)}, u32[]{:S(2)}) collective-permute-start(bf16[2,128,1024]{2,1,0:T(8,128)(2,1)} %fusion.57), channel_id=1, source_target_pairs={{0,704},{64,0},{128,64},{192,128},{256,192},{320,256},{384,320},{4... | collective-permute-start | bytes 1572872 | tf_op jit(solution)/shard_map/ppermute | solution.py:36
  152.1 8.0 %copy-start.9 = (bf16[2,128,1024]{2,1,0:T(8,128)(2,1)S(1)}, bf16[2,128,1024]{2,1,0:T(8,128)(2,1)}, u32[]{:S(2)}) copy-start(bf16[2,128,1024]{2,1,0:T(8,128)(2,1)} %copy-done.8) | copy-start | bytes 1572868
  152.1 9.1 %copy-start.11 = (bf16[2,1,512,1024]{3,2,1,0:T(8,128)(2,1)S(1)}, bf16[2,1,512,1024]{3,2,1,0:T(8,128)(2,1)}, u32[]{:S(2)}) copy-start(bf16[2,1,512,1024]{3,2,1,0:T(8,128)(2,1)} %param.11) | copy-start | bytes 6291460
  163.0 18.8 %all-to-all-start.6 = ((bf16[4,2,128,512]{3,2,1,0:T(8,128)(2,1)}), bf16[4,2,128,512]{3,2,1,0:T(8,128)(2,1)}, u32[]{:S(2)}, u32[]{:S(2)}) async-start(bf16[4,2,128,512]{3,2,1,0:T(8,128)(2,1)} %broadcast_in_dim.50), calls=%async_computation.6 | async-start | bytes 2097152 | tf_op jit(solution)/shard_map/all_to_all | solution.py:14
  167.3 121.8 %reduce-scatter.2.cloned.1.call-start = ((), (), s32[]{:S(2)}) async-start(), calls=%async_computation.9 | async-start | bytes 4456448 | tf_op jit(solution)/shard_map/reduce_scatter | solution.py:42
  167.5 2.0 copy-start.2
  167.5 2.0 copy-start.14
  169.5 1.0 copy-start.6
  170.6 4.0 %copy-start.16 = (bf16[1,128,1024]{2,1,0:T(8,128)(2,1)S(1)}, bf16[1,128,1024]{2,1,0:T(8,128)(2,1)}, u32[]{:S(2)}) copy-start(bf16[1,128,1024]{2,1,0:T(8,128)(2,1)} %copy-done.15) | copy-start | bytes 786436
  170.6 4.0 %copy-start.18 = (bf16[1,128,1024]{2,1,0:T(8,128)(2,1)S(1)}, bf16[1,128,1024]{2,1,0:T(8,128)(2,1)}, u32[]{:S(2)}) copy-start(bf16[1,128,1024]{2,1,0:T(8,128)(2,1)} %copy-done.17) | copy-start | bytes 786436
  183.2 4.7 %copy-start.3 = (bf16[2,512,1024]{2,1,0:T(8,128)(2,1)S(1)}, bf16[2,512,1024]{2,1,0:T(8,128)(2,1)}, u32[]{:S(2)}) copy-start(bf16[2,512,1024]{2,1,0:T(8,128)(2,1)} %add_convert_fusion) | copy-start | bytes 6291460
  (2 other events, 1.7 us)
Sparse Core Ops, SparseCore 0:
  190.4 98.6 reduce-scatter.1
where the time goes:
time: 299 us; the launch traced here: 298 us
  waiting for transfers between devices  162 us (54%)
  starting transfers between devices  58.9 us (20%)
  matrix products  35 us (12%)
  other arithmetic  18.8 us (6%)
  between operations  14.5 us (5%)
  local copies, waits for them, and re-layouts  8.77 us (3%)
    reduce_scatter x1, waiting for transfers between devices, sent_together(): whole = lax.psum_scatter(both, axis, scatter_dimension=dim, tiled=True)  95.7 us
    all_to_all x8, waiting for transfers between devices, from_everyone(): return lax.all_to_all(copies, axis, split_axis=0, concat_axis=0, tiled=True)  50.7 us
    all_to_all x8, starting transfers between devices, from_everyone(): return lax.all_to_all(copies, axis, split_axis=0, concat_axis=0, tiled=True)  41.1 us
    ppermute x2, starting transfers between devices, shifted(): return lax.ppermute(x, axis, [(i, (i + by) % count) for i in range(count)])  17.6 us
    ppermute x2, waiting for transfers between devices, shifted(): return lax.ppermute(x, axis, [(i, (i + by) % count) for i in range(count)])  15.3 us
    dot_general x3, matrix products, block_back(): jnp.einsum('vrk,vrd->vkd', grad_scaled, gained, preferred_element_type=jn...  12.8 us
    reduce_sum x6, other arithmetic, of_everyone(): return jnp.sum(everything.astype(jnp.float32), axis=0)  8.77 us
    broadcast_in_dim x8, local copies, waits for them, and re-layouts, from_everyone(): copies = jnp.broadcast_to(x, (lax.axis_size(axis), *x.shape))  7.77 us
  transfers between devices with their start and end apart: 11, of which 10 were waited for; matrix products, arithmetic and copies ran while one was open for 14% of the time, Pallas kernels for 0%

commit v1 on v0

v1 whole, which is shorter than its diff:
```python
import jax
import jax.numpy as jnp
from jax import lax
from jax.experimental import pallas as pl
from jax.experimental.pallas import tpu as pltpu
from jax.sharding import PartitionSpec as P

D = 4096
EPS = 1e-05
ROWS = 128
HALF = 64
DL = 1024
R = 512
STEPS = 3
SEQS = 4
F32 = jnp.float32
BF16 = jnp.bfloat16
MESH = pl.DeviceIdType.MESH

SPLITS = ((0, 768, "x"), (768, 256, "y"))
N_SEM = 208


def slope_of(values, sigma):
    return sigma * (1.0 + values * (1.0 - sigma))


def dot_nt(a, b):
    return lax.dot_general(a, b, (((1,), (1,)), ((), ())), preferred_element_type=F32)


def dot_nn(a, b):
    return lax.dot_general(a, b, (((1,), (0,)), ((), ())), preferred_element_type=F32)


def dot_tn(a, b):
    return lax.dot_general(a, b, (((0,), (0,)), ((), ())), preferred_element_type=F32)


def kernel(
    sections,
    saved_hbm, win_hbm, wout_hbm, gain, arriving_hbm, logp_hbm, rewards, lengths, ids,
    gin_hbm, gout_hbm, leaving_hbm,
    xs, win, wout, lg, call, gained, hid, gs, coef,
    part_pre, part_back, d_pre, d_back, chip_pre, chip_back, y_pre, y_back,
    sq, sq_d, sq_chip, sq_y, inv, slope, presum, cout,
    rw, rw_x, rw_sum, rw_y, weight,
    g, h1, f1, s1, h2, f2, fin,
    load_sem, store_sem, send_sem, recv_sem,
):
    sec = lax.axis_index("pipe")
    dp = lax.axis_index("dp")
    tn = lax.axis_index("tensor")
    xi = dp // 4
    yi = dp % 4
    core = tn % 2
    mine = pl.multiple_of(core * HALF, HALF)
    other = pl.multiple_of((1 - core) * HALF, HALF)
    top = sec == sections - 1

    partner = (sec, dp, tn + 1 - 2 * core)
    across = (sec, dp, (tn + 2) % 4)
    below = ((sec + sections - 1) % sections, dp, tn)
    above = ((sec + 1) % sections, dp, tn)

    def at_x(by):
        return (sec, ((xi + by) % 4) * 4 + yi, tn)

    def at_y(by):
        return (sec, xi * 4 + (yi + by) % 4, tn)

    peers = [partner, across, below, above] + [at(by) for at in (at_x, at_y) for by in (1, 2, 3)]

    used = [0]
    sends = []

    def remote(src, dst, device):
        k = used[0]
        used[0] += 1
        copy = pltpu.make_async_remote_copy(
            src_ref=src, dst_ref=dst, send_sem=send_sem.at[k], recv_sem=recv_sem.at[k],
            device_id=device, device_id_type=MESH,
        )
        copy.start()
        sends.append(copy)
        return copy

    loads = {}

    def load(name, src, dst):
        copy = pltpu.make_async_copy(src, dst, load_sem.at[len(loads)])
        copy.start()
        loads[name] = copy

    for v in range(2):
        load(("c", v), arriving_hbm.at[v], call.at[v, pl.ds(0, ROWS)])
        load(("wout", v), wout_hbm.at[v], wout.at[v])
        load(("x", 0, v), saved_hbm.at[0, v], xs.at[0, v])
        load(("win", v), win_hbm.at[v], win.at[v])
    for t in (1, 2):
        for v in range(2):
            load(("x", t, v), saved_hbm.at[t, v], xs.at[t, v])
    load("lg", logp_hbm, lg)

    barrier = pltpu.get_barrier_semaphore()
    for peer in peers:
        pl.semaphore_signal(barrier, inc=1, device_id=peer, device_id_type=MESH)

    lane = lax.broadcasted_iota(jnp.int32, (8, 128), 1)
    row = lax.broadcasted_iota(jnp.int32, (8, 128), 0)
    tile = jnp.zeros((8, 128), F32)
    for n in range(2):
        for k in range(SEQS):
            member = lane == ids[n, 0, k]
            tile = tile + jnp.where(
                member, jnp.where(row == 0, rewards[n, 0, k], jnp.where(row == 1, 1.0, 0.0)), 0.0
            )
    rw[...] = tile

    rows_of = [pl.ds(t * ROWS, ROWS) for t in range(STEPS)]

    def back_part(t, v):
        for n in range(2):
            cols = pl.ds(n * 256, 256)
            part_back[t, v, :, cols] = dot_nt(
                call[v, rows_of[t], :], wout[v, cols, :]
            ).astype(BF16)

    def back_send(t, v):
        return remote(part_back.at[t, v, pl.ds(other, HALF)], d_back.at[t, v], partner)

    def pre_part(t, v):
        gain_row = gain[v]
        slot = 0 if t == 0 else 1
        lane_no = t * 2 + v

        def body(i, carry):
            r = pl.ds(pl.multiple_of(i * 16, 16), 16)
            values = xs[t, v, r, :].astype(F32)
            gained[v, pl.ds(pl.multiple_of(t * ROWS + i * 16, 16), 16), :] = (
                values * gain_row
            ).astype(BF16)
            total = jnp.sum(values * values, axis=-1, keepdims=True)
            at = lax.broadcasted_iota(jnp.int32, (16, 128), 1) == lane_no
            sq[slot, r, :] = jnp.where(at, total, sq[slot, r, :])
            return carry

        lax.fori_loop(0, ROWS // 16, body, 0)
        for n in range(2):
            cols = pl.ds(n * 256, 256)
            part_pre[t, v, :, cols] = dot_nt(
                gained[v, rows_of[t], :], win[v, cols, :]
            ).astype(BF16)

    def pre_send(t, v):
        return remote(part_pre.at[t, v, pl.ds(other, HALF)], d_pre.at[t, v], partner)

    def chip_sum(t, v, copy, part, arrived, chip, far):
        copy.wait_recv()
        chip[t, v] = (
            part[t, v, pl.ds(mine, HALF), :].astype(F32) + arrived[t, v].astype(F32)
        ).astype(BF16)
        return remote(chip.at[t, v], far.at[t, v], across)

    def sq_chip_sum(slot, copy):
        copy.wait_recv()
        sq_chip[slot] = sq[slot, pl.ds(mine, HALF), :] + sq_d[slot]
        return remote(sq_chip.at[slot], sq_y.at[slot], across)

    def inv_of(slot, copy):
        copy.wait_recv()
        total = sq_chip[slot] + sq_y[slot]
        inv[slot] = 1.0 / jnp.sqrt(total / D + EPS)

    def inv_rows(t, v, r):
        lane_no = t * 2 + v
        return inv[0 if t == 0 else 1, r, :][:, lane_no : lane_no + 1]

    def hidden_of(t, v, copy):
        copy.wait_recv()

        def body(i, carry):
            r = pl.ds(pl.multiple_of(i * 16, 16), 16)
            total = chip_pre[t, v, r, :].astype(F32) + y_pre[t, v, r, :].astype(F32)
            pre = inv_rows(t, v, r) * total
            sigma = jax.nn.sigmoid(pre)
            presum[t, v, r, :] = total
            slope[t, v, r, :] = slope_of(pre, sigma)
            where = pl.ds(pl.multiple_of(t * ROWS + mine + i * 16, 16), 16)
            hid[v, where, :] = (pre * sigma).astype(BF16)
            return carry

        lax.fori_loop(0, HALF // 16, body, 0)
        own = pl.ds(pl.multiple_of(t * ROWS + mine, HALF), HALF)
        return remote(hid.at[v, own], hid.at[v, own], partner)

    def scaled_of(t, v, copy):
        copy.wait_recv()

        def body(i, carry):
            r = pl.ds(pl.multiple_of(i * 16, 16), 16)
            back = chip_back[t, v, r, :].astype(F32) + y_back[t, v, r, :].astype(F32)
            scale = inv_rows(t, v, r)
            grad_pre = back * slope[t, v, r, :]
            where = pl.ds(pl.multiple_of(t * ROWS + mine + i * 16, 16), 16)
            gs[v, where, :] = (scale * grad_pre).astype(BF16)
            radial = jnp.sum(grad_pre * presum[t, v, r, :], axis=-1, keepdims=True)
            amount = scale * scale * scale * radial / D
            here = pl.ds(pl.multiple_of(mine + i * 16, 16), 16)
            coef[t, v, here, :] = jnp.broadcast_to(amount, (16, 128))
            return carry

        lax.fori_loop(0, HALF // 16, body, 0)
        own = pl.ds(pl.multiple_of(t * ROWS + mine, HALF), HALF)
        here = pl.ds(mine, HALF)
        return (
            remote(gs.at[v, own], gs.at[v, own], partner),
            remote(coef.at[t, v, here], coef.at[t, v, here], partner),
        )

    def cot_out(t, v, copies):
        for copy in copies:
            copy.wait_recv()
        amount = coef[t, v]
        for n in range(4):
            cols = pl.ds(n * 256, 256)
            product = dot_nn(gs[v, rows_of[t], :], win[v, :, cols])
            out = (
                call[v, rows_of[t], cols].astype(F32)
                + gain[v, :, cols] * product
                - xs[t, v, :, cols].astype(F32) * amount[:, :1]
            )
            cout[t, v, :, cols] = out.astype(BF16)

    def shift(t, v):
        k = t * 2 + v
        slot = v if v == 0 else jnp.where(sec == 0, 0, 1)
        copy = pltpu.make_async_remote_copy(
            src_ref=cout.at[t, v], dst_ref=call.at[slot, rows_of[t + 1]],
            send_sem=send_sem.at[N_SEM - 4 + k], recv_sem=recv_sem.at[N_SEM - 4 + t * 2 + slot],
            device_id=below, device_id_type=MESH,
        )
        if v == 1:
            copy.start()
        else:
            @pl.when(sec != 0)
            def _():
                copy.start()

        return copy

    def shift_in(t, v):
        slot_ref = call.at[v, rows_of[t + 1]]
        copy = pltpu.make_async_remote_copy(
            src_ref=slot_ref, dst_ref=slot_ref,
            send_sem=send_sem.at[N_SEM - 4 + t * 2 + v], recv_sem=recv_sem.at[N_SEM - 4 + t * 2 + v],
            device_id=below, device_id_type=MESH,
        )
        if v == 0:
            copy.wait_recv()
        else:
            @pl.when(jnp.logical_not(top))
            def _():
                copy.wait_recv()

    class Ring:
        def __init__(self, p, kind, v, first, width, axis):
            self.p, self.kind, self.v = p, kind, v
            self.cols = pl.ds(first, width)
            if axis == "x":
                self.axes = ((xi, at_x), (yi, at_y))
                self.chunk = lambda j, lo, n: g.at[p, j, pl.ds(lo, n), :, self.cols]
            else:
                self.axes = ((yi, at_y), (xi, at_x))
                self.chunk = lambda j, lo, n: g.at[p, pl.ds(lo, n), j, :, self.cols]

        def start(self, phase):
            i, at = self.axes[phase]
            nxt, prv = at(1), at(3)
            far, up, down = (i + 2) % 4, (i + 1) % 4, (i + 3) % 4
            c = self.cols
            if phase == 0:
                src, n = self.chunk, 2
                half = lambda d: h1.at[self.p, d, :, :, c]
                full = lambda d, lo: f1.at[self.p, d, pl.ds(lo, 2), :, c]
            else:
                src = lambda j, lo, n: s1.at[self.p, j, pl.ds(lo, n), c]
                n = 16
                half = lambda d: h2.at[self.p, d, :, c]
                full = lambda d, lo: f2.at[self.p, d, pl.ds(lo, 16), c]
            self.src, self.n, self.full = src, n, full
            self.half_a = remote(src(far, 0, n), half(0), nxt)
            self.half_b = remote(src(far, n, n), half(1), prv)
            self.plain = [
                remote(src(up, n, n), full(0, n), nxt),
                remote(src(down, 0, n), full(1, 0), prv),
            ]

        def merge(self, phase):
            i, at = self.axes[phase]
            nxt, prv = at(1), at(3)
            up, down = (i + 1) % 4, (i + 3) % 4
            n = self.n
            for d, copy, j, lo in ((0, self.half_a, up, 0), (1, self.half_b, down, n)):
                copy.wait_recv()
                chunk = self.src(j, lo, n)
                arrived = (h1 if phase == 0 else h2).at[self.p, d]
                if phase == 0:
                    arrived = arrived.at[:, :, self.cols]
                else:
                    arrived = arrived.at[:, self.cols]
                chunk[...] = (chunk[...].astype(F32) + arrived[...].astype(F32)).astype(BF16)
                self.plain.append(remote(chunk, self.full(d, lo), (nxt, prv)[d]))

        def middle(self):
            for copy in self.plain:
                copy.wait_recv()
            i = self.axes[0][0]
            for k in range(4):
                own = self.chunk(i, k, 1)
                total = own[...].reshape(32, -1).astype(F32)
                for d in range(2):
                    total = total + f1[self.p, d, k, :, self.cols].astype(F32)
                s1[self.p, k, :, self.cols] = total.astype(BF16)
            self.start(1)

        def end(self):
            for copy in self.plain:
                copy.wait_recv()
            i = self.axes[1][0]
            total = s1[self.p, i, :, self.cols].astype(F32)
            for d in range(2):
                total = total + f2[self.p, d, :, self.cols].astype(F32)
            fin[self.kind, self.v, :, self.cols] = total * (1.0 / (16 * ROWS))

    stores = []

    def store(src, dst):
        copy = pltpu.make_async_copy(src, dst, store_sem.at[len(stores)])
        copy.start()
        stores.append(copy)

    class Piece:
        def __init__(self, p, kind, v):
            self.p, self.kind, self.v = p, kind, v
            self.rings = [Ring(p, kind, v, *split) for split in SPLITS]

        def start(self):
            left, right = ((gs, gained), (hid, call))[self.kind]
            v, p = self.v, self.p

            def body(m, carry):
                j = (xi + 2 + m) % 4
                lhs = left[v, :, pl.ds(pl.multiple_of(j * 128, 128), 128)]
                for n in range(4):
                    cols = pl.ds(n * 256, 256)
                    block = dot_tn(lhs, right[v, :, cols]).astype(BF16)
                    g[p, j, :, :, cols] = block.reshape(4, 32, 256)
                return carry

            lax.fori_loop(0, 4, body, 0)
            for ring in self.rings:
                ring.start(0)

        def merge(self, phase):
            for ring in self.rings:
                ring.merge(phase)

        def middle(self):
            for ring in self.rings:
                ring.middle()

        def end(self):
            for ring in self.rings:
                ring.end()
            store(fin.at[self.kind, self.v], (gin_hbm, gout_hbm)[self.kind].at[self.v])

    loads[("c", 0)].wait()
    loads[("wout", 0)].wait()
    back_part(0, 0)
    pl.semaphore_wait(barrier, len(peers))
    pre_copy, back_copy, sq_copy = {}, {}, {}
    back_copy[0, 0] = back_send(0, 0)
    rw_copies = [remote(rw, rw_x.at[by - 1], at_x(by)) for by in (1, 2, 3)]
    sq[...] = jnp.zeros_like(sq)
    loads[("x", 0, 0)].wait()
    loads[("win", 0)].wait()
    pre_part(0, 0)
    pre_copy[0, 0] = pre_send(0, 0)
    loads[("c", 1)].wait()
    loads[("wout", 1)].wait()
    back_part(0, 1)
    back_copy[0, 1] = back_send(0, 1)
    loads[("x", 0, 1)].wait()
    loads[("win", 1)].wait()
    pre_part(0, 1)
    pre_copy[0, 1] = pre_send(0, 1)
    sq_copy[0] = remote(sq.at[0, pl.ds(other, HALF)], sq_d.at[0], partner)

    def back_chip(t, v):
        back_copy[t, v] = chip_sum(t, v, back_copy[t, v], part_back, d_back, chip_back, y_back)

    def pre_chip(t, v):
        pre_copy[t, v] = chip_sum(t, v, pre_copy[t, v], part_pre, d_pre, chip_pre, y_pre)

    back_chip(0, 0)
    pre_chip(0, 0)
    sq_copy[0] = sq_chip_sum(0, sq_copy[0])
    back_chip(0, 1)
    pre_chip(0, 1)
    for t in (1, 2):
        for v in range(2):
            loads[("x", t, v)].wait()
            pre_part(t, v)
            pre_copy[t, v] = pre_send(t, v)
    sq_copy[1] = remote(sq.at[1, pl.ds(other, HALF)], sq_d.at[1], partner)
    for copy in rw_copies:
        copy.wait_recv()
    rw_sum[...] = rw[...] + rw_x[0] + rw_x[1] + rw_x[2]
    rw_copies = [remote(rw_sum, rw_y.at[by - 1], at_y(by)) for by in (1, 2, 3)]

    inv_of(0, sq_copy[0])
    hid_copy, gs_copy = {}, {}
    for v in range(2):
        hid_copy[0, v] = hidden_of(0, v, pre_copy[0, v])
        gs_copy[0, v] = scaled_of(0, v, back_copy[0, v])
    shifts = []
    for v in range(2):
        cot_out(0, v, gs_copy[0, v])
        shifts.append(shift(0, v))

    sq_copy[1] = sq_chip_sum(1, sq_copy[1])
    for t in (1, 2):
        for v in range(2):
            pre_chip(t, v)
    loads["lg"].wait()
    for copy in rw_copies:
        copy.wait_recv()
    sums = rw_sum[...] + rw_y[0] + rw_y[1] + rw_y[2]
    means = sums[0:1, :] / jnp.maximum(sums[1:2, :], 1.0)
    position = lax.broadcasted_iota(jnp.int32, (ROWS, 128), 0)
    for n in range(2):
        begin = jnp.int32(0)
        weights = jnp.zeros((ROWS, 128), F32)
        for k in range(SEQS):
            finish = begin + lengths[n, 0, k]
            own = jnp.sum(
                jnp.where(lane[0:1, :] == ids[n, 0, k], means, 0.0), axis=-1, keepdims=True
            )
            advantage = rewards[n, 0, k] - own
            inside = jnp.logical_and(position >= begin, position < finish)
            weights = weights + jnp.where(inside, advantage, 0.0)
            begin = finish
        weight[n] = -weights

    @pl.when(top)
    def _():
        for n in range(2):
            def body(i, carry):
                r = pl.ds(pl.multiple_of(i * 16, 16), 16)
                to = pl.ds(pl.multiple_of((n + 1) * ROWS + i * 16, 16), 16)
                call[1, to, :] = (weight[n, r, :][:, :1] * lg[n, r, :].astype(F32)).astype(BF16)
                return carry

            lax.fori_loop(0, ROWS // 16, body, 0)

    inv_of(1, sq_copy[1])
    for t in (1, 2):
        for v in range(2):
            hid_copy[t, v] = hidden_of(t, v, pre_copy[t, v])

    for v in range(2):
        shift_in(0, v)
        back_part(1, v)
        back_copy[1, v] = back_send(1, v)
        back_chip(1, v)
        gs_copy[1, v] = scaled_of(1, v, back_copy[1, v])
        cot_out(1, v, gs_copy[1, v])
        shifts.append(shift(1, v))
    for t in range(STEPS):
        for v in range(2):
            hid_copy[t, v].wait_recv()

    out_piece = [Piece(0, 1, 0), Piece(2, 1, 1)]
    in_piece = [Piece(1, 0, 0), Piece(3, 0, 1)]

    shift_in(1, 0)
    back_part(2, 0)
    back_copy[2, 0] = back_send(2, 0)
    out_piece[0].start()
    back_chip(2, 0)
    gs_copy[2, 0] = scaled_of(2, 0, back_copy[2, 0])
    cot_out(2, 0, gs_copy[2, 0])
    store(cout.at[2, 0], leaving_hbm.at[0])
    in_piece[0].start()
    out_piece[0].merge(0)
    shift_in(1, 1)
    back_part(2, 1)
    back_copy[2, 1] = back_send(2, 1)
    out_piece[1].start()
    back_chip(2, 1)
    in_piece[0].merge(0)
    gs_copy[2, 1] = scaled_of(2, 1, back_copy[2, 1])
    cot_out(2, 1, gs_copy[2, 1])
    store(cout.at[2, 1], leaving_hbm.at[1])
    in_piece[1].start()
    out_piece[1].merge(0)
    out_piece[0].middle()
    in_piece[1].merge(0)
    out_piece[0].merge(1)
    in_piece[0].middle()
    in_piece[0].merge(1)
    out_piece[0].end()
    out_piece[1].middle()
    out_piece[1].merge(1)
    in_piece[0].end()
    in_piece[1].middle()
    in_piece[1].merge(1)
    out_piece[1].end()
    in_piece[1].end()

    for copy in sends:
        copy.wait_send()

    @pl.when(sec != 0)
    def _():
        shifts[0].wait_send()
        shifts[2].wait_send()

    shifts[1].wait_send()
    shifts[3].wait_send()
    for copy in stores:
        copy.wait()
    assert used[0] <= N_SEM - 4, used[0]


def shards(saved, proj_in, proj_out, gain, arriving, logp, rewards, lengths, ids):
    sections = lax.axis_size("pipe")
    any_spec = pl.BlockSpec(memory_space=pl.ANY)
    vmem = pl.BlockSpec(memory_space=pltpu.VMEM)
    smem = pl.BlockSpec(memory_space=pltpu.SMEM)
    V = pltpu.VMEM
    grad_in, grad_out, leaving = pl.pallas_call(
        lambda *refs: kernel(sections, *refs),
        name="window",
        out_shape=(
            jax.ShapeDtypeStruct((2, 32, DL), F32),
            jax.ShapeDtypeStruct((2, 32, DL), F32),
            jax.ShapeDtypeStruct((2, ROWS, DL), BF16),
        ),
        in_specs=[any_spec, any_spec, any_spec, vmem, any_spec, any_spec, smem, smem, smem],
        out_specs=(any_spec, any_spec, any_spec),
        scratch_shapes=[
            V((STEPS, 2, ROWS, DL), BF16),
            V((2, R, DL), BF16),
            V((2, R, DL), BF16),
            V((2, ROWS, DL), BF16),
            V((2, STEPS * ROWS, DL), BF16),
            V((2, STEPS * ROWS, DL), BF16),
            V((2, STEPS * ROWS, R), BF16),
            V((2, STEPS * ROWS, R), BF16),
            V((STEPS, 2, ROWS, 128), F32),
            V((STEPS, 2, ROWS, R), BF16),
            V((STEPS, 2, ROWS, R), BF16),
            V((STEPS, 2, HALF, R), BF16),
            V((STEPS, 2, HALF, R), BF16),
            V((STEPS, 2, HALF, R), BF16),
            V((STEPS, 2, HALF, R), BF16),
            V((STEPS, 2, HALF, R), BF16),
            V((STEPS, 2, HALF, R), BF16),
            V((2, ROWS, 128), F32),
            V((2, HALF, 128), F32),
            V((2, HALF, 128), F32),
            V((2, HALF, 128), F32),
            V((2, HALF, 128), F32),
            V((STEPS, 2, HALF, R), F32),
            V((STEPS, 2, HALF, R), F32),
            V((STEPS, 2, ROWS, DL), BF16),
            V((8, 128), F32),
            V((3, 8, 128), F32),
            V((8, 128), F32),
            V((3, 8, 128), F32),
            V((2, ROWS, 128), F32),
            V((4, 4, 4, 32, DL), BF16),
            V((4, 2, 2, 32, DL), BF16),
            V((4, 2, 4, 32, DL), BF16),
            V((4, 4, 32, DL), BF16),
            V((4, 2, 16, DL), BF16),
            V((4, 2, 32, DL), BF16),
            V((2, 2, 32, DL), F32),
            pltpu.SemaphoreType.DMA((16,)),
            pltpu.SemaphoreType.DMA((8,)),
            pltpu.SemaphoreType.DMA((N_SEM,)),
            pltpu.SemaphoreType.DMA((N_SEM,)),
        ],
        compiler_params=pltpu.CompilerParams(
            collective_id=0, has_side_effects=True, vmem_limit_bytes=60 * 2**20
        ),
    )(
        saved[:, :, 0], proj_in[:, 0], proj_out[:, 0], gain, arriving[:, 0], logp,
        rewards, lengths, ids,
    )
    return grad_in[:, None], grad_out[:, None], leaving[:, None]


def solution(mesh):
    return jax.shard_map(
        shards,
        mesh=mesh,
        in_specs=(
            P(None, None, "pipe", "dp", "tensor"),
            P(None, "pipe", None, "tensor"),
            P(None, "pipe", None, "tensor"),
            P(None, "pipe", "tensor"),
            P(None, "pipe", "dp", "tensor"),
            P(None, "dp", "tensor"),
            P(None, "dp", None),
            P(None, "dp", None),
            P(None, "dp", None),
        ),
        out_specs=(
            P(None, "pipe", "dp", "tensor"),
            P(None, "pipe", "dp", "tensor"),
            P(None, "pipe", "dp", "tensor"),
        ),
        check_vma=False,
    )
```

time: 299 us -> 117 us (0.39)
  the two profiles are of different devices: /device:TPU:2 before, /device:TPU:4 now
where the time goes in v1:
time: 117 us; the launch traced here: 116 us
  Pallas kernels  110 us (94%)
  local copies, waits for them, and re-layouts  5.21 us (4%)
    pallas_call x1, Pallas kernels, shards(): pl.pallas_call(lambda *refs: kernel(sections, *refs), name='window', out_...  110 us
    unnamed x3, local copies, waits for them, and re-layouts  5.21 us

profile of v1, /device:TPU:4, one launch (start us, length us, event | category | flops | bytes accessed | tf_op | source)
XLA Modules:
  0.0 116.2 jit_solution(2150885382867570432)
XLA Ops:
  0.6 110.4 %window.1 = (f32[2,32,1024]{2,1,0:T(8,128)}, f32[2,32,1024]{2,1,0:T(8,128)}, bf16[2,128,1024]{2,1,0:T(8,128)(2,1)}) custom-call(bf16[3,2,128,1024]{3,2,1,0:T(8,128)(2,1)} %bitcast.15, bf16[2,512,1024]{2,1,0:T(8,128)(2,1)} %bitcast.13, bf16[2,512,1024]{2,1,0:T(8,128)(2,1)} %bitcast.14, f32[2,1,1024]{2,1,0:T(1,128)} %refs_3_.1, ...), custom_call_target="tpu_custom_call" | custom-call | tf_op jit(solution)/shard_map/window/pallas_call | solution.py:543
  111.0 1.7 %copy.18 = f32[2,1,32,1024]{3,2,1,0:T(8,128)} copy(f32[2,1,32,1024]{3,2,1,0:T(8,128)} %bitcast.19) | data formatting | bytes 524288
  112.7 1.7 %copy.19 = f32[2,1,32,1024]{3,2,1,0:T(8,128)} copy(f32[2,1,32,1024]{3,2,1,0:T(8,128)} %bitcast.18) | data formatting | bytes 524288
  114.4 1.9 %copy.20 = bf16[2,1,128,1024]{3,2,1,0:T(8,128)(2,1)} copy(bf16[2,1,128,1024]{3,2,1,0:T(8,128)(2,1)} %bitcast.16) | data formatting | bytes 1048576

commit v2 on v0

v2 whole, which is shorter than its diff:
```python
import jax
import jax.numpy as jnp
from jax import lax
from jax.experimental import pallas as pl
from jax.experimental.pallas import tpu as pltpu
from jax.sharding import PartitionSpec as P

D = 4096
EPS = 1e-05
ROWS = 128
HALF = 64
DL = 1024
R = 512
STEPS = 3
SEQS = 4
F32 = jnp.float32
BF16 = jnp.bfloat16
MESH = pl.DeviceIdType.MESH

SPLITS = ((0, 768, "x"), (768, 256, "y"))
N_RECV = 96
N_SEND = 32
scope = jax.named_scope


def dot_nt(a, b):
    return lax.dot_general(a, b, (((1,), (1,)), ((), ())), preferred_element_type=F32)


def dot_nn(a, b):
    return lax.dot_general(a, b, (((1,), (0,)), ((), ())), preferred_element_type=F32)


def dot_tn(a, b):
    return lax.dot_general(a, b, (((0,), (0,)), ((), ())), preferred_element_type=F32)


def kernel(
    sections,
    saved_hbm, win_hbm, wout_hbm, gain_hbm, arriving_hbm, logp_hbm, rewards_hbm, lengths_hbm, ids_hbm,
    gin, gout, leaving,
    xs, win, wout, gain, lg, call, gained, hid, gs, coef,
    part_pre, part_back, d_pre, d_back, chip_pre, chip_back, y_pre, y_back,
    sqp, sq, sq_d, sq_chip, sq_y, inv, slope, presum, cout,
    rw, rw_in, weight, rewards, lengths, ids,
    g, h1, f1, s1, h2, f2,
    load_sem, send_sem, recv_sem, shift_send, shift_recv,
):
    sec = lax.axis_index("pipe")
    dp = lax.axis_index("dp")
    tn = lax.axis_index("tensor")
    xi = dp // 4
    yi = dp % 4
    core = tn % 2
    mine = pl.multiple_of(core * HALF, HALF)
    other = pl.multiple_of((1 - core) * HALF, HALF)
    top = sec == sections - 1
    early = [jnp.where(sec == 0, 1 - a, a) for a in range(2)]
    late = [jnp.where(top, 1 - a, a) for a in range(2)]
    block = [early, early, late]

    partner = (sec, dp, tn + 1 - 2 * core)
    across = (sec, dp, (tn + 2) % 4)
    below = ((sec + sections - 1) % sections, dp, tn)
    above = ((sec + 1) % sections, dp, tn)

    def at_x(to):
        return (sec, to * 4 + yi, tn)

    def at_y(to):
        return (sec, xi * 4 + to, tn)

    def ring(i, by):
        return (i + by) % 4

    peers = [partner, across, below, above]
    peers += [at_x(ring(xi, 1)), at_x(ring(xi, 3)), at_y(ring(yi, 1)), at_y(ring(yi, 3))]
    barrier = pltpu.get_barrier_semaphore()
    for peer in peers:
        pl.semaphore_signal(barrier, inc=1, device_id=peer, device_id_type=MESH)

    recv_used = [0]
    classes = {}

    def recv_slot():
        recv_used[0] += 1
        return recv_sem.at[recv_used[0] - 1]

    def send_slot(name, whole):
        if name not in classes:
            classes[name] = (send_sem.at[len(classes)], whole)
        return classes[name][0]

    def remote(src, dst, device, name, whole, recv=None):
        copy = pltpu.make_async_remote_copy(
            src_ref=src, dst_ref=dst, send_sem=send_slot(name, whole),
            recv_sem=recv_slot() if recv is None else recv,
            device_id=device, device_id_type=MESH,
        )
        copy.start()
        return copy

    def arrived(whole, recv):
        pltpu.make_async_remote_copy(
            src_ref=whole, dst_ref=whole, send_sem=send_sem.at[0], recv_sem=recv,
            device_id=partner, device_id_type=MESH,
        ).wait_recv()

    loads = {}

    def load(name, src, dst):
        copy = pltpu.make_async_copy(src, dst, load_sem.at[len(loads)])
        copy.start()
        loads[name] = copy

    load("gain", gain_hbm, gain)
    for a in range(2):
        v = early[a]
        load(("x", 0, a), saved_hbm.at[0, v], xs.at[0, v])
        load(("win", a), win_hbm.at[v], win.at[v])
        load(("c", a), arriving_hbm.at[v], call.at[v, pl.ds(0, ROWS)])
        load(("wout", a), wout_hbm.at[v], wout.at[v])
    for t in (1, 2):
        for a in range(2):
            load(("x", t, a), saved_hbm.at[t, block[t][a]], xs.at[t, block[t][a]])
    load("rewards", rewards_hbm, rewards)
    load("lengths", lengths_hbm, lengths)
    load("ids", ids_hbm, ids)
    load("lg", logp_hbm, lg)

    rows_of = [pl.ds(t * ROWS, ROWS) for t in range(STEPS)]

    def sixteen(start):
        return pl.ds(pl.multiple_of(start, 16), 16)

    back_copy, pre_copy, sq_copy, hid_copy, gs_copy = {}, {}, {}, {}, {}

    def back_part(t, a):
        v = block[t][a]
        with scope(f"back_part{t}{a}"):
            for n in range(2):
                cols = pl.ds(n * 256, 256)
                part_back[t, a, :, cols] = dot_nt(
                    call[v, rows_of[t], :], wout[v, cols, :]
                ).astype(BF16)

    def back_send(t, a):
        back_copy[t, a] = remote(
            part_back.at[t, a, pl.ds(other, HALF)], d_back.at[t, a], partner, "back", d_back
        )

    def pre_part(t, a):
        v = block[t][a]
        with scope(f"pre_part{t}{a}"):
            gain_row = gain[v]

            def body(i, carry):
                values = xs[t, v, sixteen(i * 16), :].astype(F32)
                gained[v, sixteen(t * ROWS + i * 16), :] = (values * gain_row).astype(BF16)
                squares = values * values
                part = squares[:, 0:128]
                for k in range(1, DL // 128):
                    part = part + squares[:, k * 128 : (k + 1) * 128]
                sqp[sixteen(i * 16), :] = part
                return carry

            lax.fori_loop(0, ROWS // 16, body, 0, unroll=2)
            for n in range(2):
                cols = pl.ds(n * 256, 256)
                part_pre[t, a, :, cols] = dot_nt(
                    gained[v, rows_of[t], :], win[v, cols, :]
                ).astype(BF16)
            total = jnp.sum(sqp[...], axis=-1, keepdims=True)
            same = lax.broadcasted_iota(jnp.int32, (ROWS, 128), 0) == lax.broadcasted_iota(
                jnp.int32, (ROWS, 128), 1
            )
            row = jnp.sum(jnp.where(same, total, 0.0), axis=0, keepdims=True)
            sq[t, a] = jnp.broadcast_to(row, (8, 128))

    def pre_send(t, a):
        pre_copy[t, a] = remote(
            part_pre.at[t, a, pl.ds(other, HALF)], d_pre.at[t, a], partner, "pre", d_pre
        )
        sq_copy[t, a] = remote(sq.at[t, a], sq_d.at[t, a], partner, "sq", sq_d)

    def chip_sum(t, a, copy, part, came, chip, far, name):
        copy.wait_recv()
        chip[t, a] = (
            part[t, a, pl.ds(mine, HALF), :].astype(F32) + came[t, a].astype(F32)
        ).astype(BF16)
        return remote(chip.at[t, a], far.at[t, a], across, name, far)

    def back_chip(t, a):
        with scope(f"back_chip{t}{a}"):
            back_copy[t, a] = chip_sum(
                t, a, back_copy[t, a], part_back, d_back, chip_back, y_back, "far_back"
            )

    def pre_chip(t, a):
        with scope(f"pre_chip{t}{a}"):
            pre_copy[t, a] = chip_sum(
                t, a, pre_copy[t, a], part_pre, d_pre, chip_pre, y_pre, "far_pre"
            )
            sq_copy[t, a].wait_recv()
            sq_chip[t, a] = sq[t, a] + sq_d[t, a]
            sq_copy[t, a] = remote(sq_chip.at[t, a], sq_y.at[t, a], across, "far_sq", sq_y)

    def hidden_of(t, a):
        v = block[t][a]
        with scope(f"hid_wait{t}{a}"):
            sq_copy[t, a].wait_recv()
            pre_copy[t, a].wait_recv()
        with scope(f"hidden{t}{a}"):
            total = sq_chip[t, a] + sq_y[t, a]
            inv_row = (1.0 / jnp.sqrt(total / D + EPS))[0:1, :]
            lane = lax.broadcasted_iota(jnp.int32, (HALF, 128), 1)
            line = lax.broadcasted_iota(jnp.int32, (HALF, 128), 0)
            scale = jnp.sum(jnp.where(lane == line + mine, inv_row, 0.0), axis=-1, keepdims=True)
            inv[t, a] = jnp.broadcast_to(scale, (HALF, 128))

            def body(i, carry):
                r = sixteen(i * 16)
                total = chip_pre[t, a, r, :].astype(F32) + y_pre[t, a, r, :].astype(F32)
                pre = inv[t, a, r, 0:1] * total
                sigma = jax.nn.sigmoid(pre)
                presum[t, a, r, :] = total
                slope[t, a, r, :] = sigma * (1.0 + pre * (1.0 - sigma))
                hid[v, sixteen(t * ROWS + mine + i * 16), :] = (pre * sigma).astype(BF16)
                return carry

            lax.fori_loop(0, HALF // 16, body, 0, unroll=True)
            own = pl.ds(pl.multiple_of(t * ROWS + mine, HALF), HALF)
            hid_copy[t, a] = remote(hid.at[v, own], hid.at[v, own], partner, "hid", d_pre)

    def scaled_of(t, a):
        v = block[t][a]
        with scope(f"gs_wait{t}{a}"):
            back_copy[t, a].wait_recv()
        with scope(f"scaled{t}{a}"):

            def body(i, carry):
                r = sixteen(i * 16)
                back = chip_back[t, a, r, :].astype(F32) + y_back[t, a, r, :].astype(F32)
                scale = inv[t, a, r, 0:1]
                grad_pre = back * slope[t, a, r, :]
                gs[v, sixteen(t * ROWS + mine + i * 16), :] = (scale * grad_pre).astype(BF16)
                radial = jnp.sum(grad_pre * presum[t, a, r, :], axis=-1, keepdims=True)
                amount = scale * scale * scale * radial / D
                coef[t, a, sixteen(mine + i * 16), :] = jnp.broadcast_to(amount, (16, 128))
                return carry

            lax.fori_loop(0, HALF // 16, body, 0, unroll=True)
            own = pl.ds(pl.multiple_of(t * ROWS + mine, HALF), HALF)
            here = pl.ds(mine, HALF)
            gs_copy[t, a] = (
                remote(gs.at[v, own], gs.at[v, own], partner, "gs", d_pre),
                remote(
                    coef.at[t, a, here], coef.at[t, a, here], partner, "coef",
                    coef.at[:, :, pl.ds(0, HALF)],
                ),
            )

    def gs_wait(t, a):
        with scope(f"gs_come{t}{a}"):
            for copy in gs_copy[t, a]:
                copy.wait_recv()

    def cot_out(t, a):
        v = block[t][a]
        with scope(f"cot_out{t}{a}"):
            amount = coef[t, a]
            for n in range(4):
                cols = pl.ds(n * 256, 256)
                product = dot_nn(gs[v, rows_of[t], :], win[v, :, cols])
                out = (
                    call[v, rows_of[t], cols].astype(F32)
                    + gain[v, :, cols] * product
                    - xs[t, v, :, cols].astype(F32) * amount[:, :1]
                ).astype(BF16)
                if t < STEPS - 1:
                    cout[t, a, :, cols] = out
                else:
                    leaving[v, :, cols] = out

    def shift_copy(t, a):
        return pltpu.make_async_remote_copy(
            src_ref=cout.at[t, a], dst_ref=call.at[a, rows_of[t + 1]],
            send_sem=shift_send.at[t * 2 + a], recv_sem=shift_recv.at[t * 2 + a],
            device_id=below, device_id_type=MESH,
        )

    def shift(t, a):
        if a == 0:
            shift_copy(t, a).start()
        else:
            @pl.when(sec != 0)
            def _():
                shift_copy(t, a).start()

    def shift_in(t, a):
        v = block[t][a]
        with scope(f"shift_in{t}{a}"):

            @pl.when(jnp.logical_not(jnp.logical_and(top, v == 1)))
            def _():
                arrived(call.at[v, rows_of[t]], shift_recv.at[(t - 1) * 2 + v])

    class Ring:
        def __init__(self, p, out, v, first, width, axis):
            self.p, self.out, self.v = p, out, v
            self.first, self.width = first, width
            self.name = f"{p}{axis}"
            cols = self.cols = pl.ds(first, width)
            pair = ((xi, at_x), (yi, at_y))
            if axis == "x":
                self.axes = pair
                chunk = lambda j, lo, n: g.at[p, j, pl.ds(lo, n), :, cols]
            else:
                self.axes = pair[::-1]
                chunk = lambda j, lo, n: g.at[p, pl.ds(lo, n), j, :, cols]
            small = lambda j, lo, n: s1.at[p, j, pl.ds(lo, n), cols]
            self.chunk = (chunk, small)
            self.n = (2, 16)
            self.half = (h1.at[p, :, :, :, cols], h2.at[p, :, :, cols])
            self.full = (f1.at[p, :, :, :, cols], f2.at[p, :, :, cols])
            self.half_recv = [recv_slot() for _ in range(2)]
            self.full_recv = [recv_slot() for _ in range(2)]

        def go(self, phase, j, lo, d, full):
            i, at = self.axes[phase]
            n = self.n[phase]
            src = self.chunk[phase](j, lo, n)
            to = at(ring(i, (1, 3)[d]))
            if full:
                dst = self.full[phase].at[d, pl.ds(lo, n)]
                remote(src, dst, to, f"f{phase}", (f1, f2)[phase], self.full_recv[phase])
            else:
                dst = self.half[phase].at[d]
                remote(src, dst, to, f"h{phase}", (h1, h2)[phase], self.half_recv[phase])

        def h(self, phase):
            far, n = ring(self.axes[phase][0], 2), self.n[phase]
            self.go(phase, far, 0, 0, False)
            self.go(phase, far, n, 1, False)

        def f(self, phase):
            i, n = self.axes[phase][0], self.n[phase]
            self.go(phase, ring(i, 1), n, 0, True)
            self.go(phase, ring(i, 3), 0, 1, True)

        def m(self, phase):
            i, n = self.axes[phase][0], self.n[phase]
            with scope(f"m{phase}_{self.name}"):
                arrived(self.half[phase], self.half_recv[phase])
                for d, j, lo in ((0, ring(i, 1), 0), (1, ring(i, 3), n)):
                    chunk = self.chunk[phase](j, lo, n)
                    came = self.half[phase].at[d]
                    chunk[...] = (chunk[...].astype(F32) + came[...].astype(F32)).astype(BF16)
                    self.go(phase, j, lo, d, True)

        def middle(self):
            with scope(f"mid_{self.name}"):
                arrived(self.full[0], self.full_recv[0])
                i = self.axes[0][0]
                for k in range(4):
                    total = self.chunk[0](i, k, 1)[...].reshape(32, self.width).astype(F32)
                    for d in range(2):
                        total = total + f1[self.p, d, k, :, self.cols].astype(F32)
                    s1[self.p, k, :, self.cols] = total.astype(BF16)
                self.h(1)
                self.f(1)

        def end(self):
            with scope(f"end_{self.name}"):
                arrived(self.full[1], self.full_recv[1])
                total = s1[self.p, self.axes[1][0], :, self.cols].astype(F32)
                for d in range(2):
                    total = total + f2[self.p, d, :, self.cols].astype(F32)
                self.out[self.v, :, self.cols] = total * (1.0 / (16 * ROWS))

    def piece(p, out, left, right, a):
        v = block[2][a]
        rings = [Ring(p, out, v, *split) for split in SPLITS]

        def compute(ring_):
            with scope(f"grad_{ring_.name}"):
                lhs = left[v]
                for k in range(ring_.width // 256):
                    cols = pl.ds(ring_.first + k * 256, 256)
                    made = dot_tn(lhs, right[v, :, cols]).astype(BF16)
                    g[p, :, :, :, cols] = made.reshape(4, 4, 32, 256)

        for ring_ in rings:
            ring_.compute = lambda ring_=ring_: compute(ring_)
        return rings

    loads["gain"].wait()
    loads[("x", 0, 0)].wait()
    loads[("win", 0)].wait()
    pre_part(0, 0)
    loads[("c", 0)].wait()
    loads[("wout", 0)].wait()
    back_part(0, 0)
    with scope("barrier"):
        pl.semaphore_wait(barrier, len(peers))
    pre_send(0, 0)
    back_send(0, 0)
    loads[("x", 0, 1)].wait()
    loads[("win", 1)].wait()
    pre_part(0, 1)
    pre_send(0, 1)
    pre_chip(0, 0)
    back_chip(0, 0)
    loads[("c", 1)].wait()
    loads[("wout", 1)].wait()
    back_part(0, 1)
    back_send(0, 1)
    pre_chip(0, 1)

    for name in ("rewards", "lengths", "ids"):
        loads[name].wait()
    lane = lax.broadcasted_iota(jnp.int32, (8, 128), 1)
    line = lax.broadcasted_iota(jnp.int32, (8, 128), 0)
    tile = jnp.zeros((8, 128), F32)
    for n in range(2):
        for k in range(SEQS):
            member = lane == ids[n, 0, k]
            amount = jnp.where(line == 0, rewards[n, 0, k], jnp.where(line == 1, 1.0, 0.0))
            tile = tile + jnp.where(member, amount, 0.0)
    rw[0] = tile
    partners = [at_x(xi + 1 - 2 * (xi % 2)), at_x(3 - xi), at_y(yi + 1 - 2 * (yi % 2)), at_y(3 - yi)]

    def rw_send(k):
        return remote(rw.at[k], rw_in.at[k], partners[k], "rw", rw_in)

    def rw_add(k, copy):
        copy.wait_recv()
        rw[k + 1] = rw[k] + rw_in[k]

    rw_copy = rw_send(0)
    back_chip(0, 1)
    loads[("x", 1, 0)].wait()
    pre_part(1, 0)
    pre_send(1, 0)
    hidden_of(0, 0)
    scaled_of(0, 0)
    pre_chip(1, 0)
    gs_wait(0, 0)
    cot_out(0, 0)
    shift(0, 0)
    rw_add(0, rw_copy)
    rw_copy = rw_send(1)
    loads[("x", 1, 1)].wait()
    pre_part(1, 1)
    pre_send(1, 1)
    hidden_of(0, 1)
    scaled_of(0, 1)
    pre_chip(1, 1)
    gs_wait(0, 1)
    cot_out(0, 1)
    shift(0, 1)

    rw_add(1, rw_copy)
    rw_copy = rw_send(2)
    for a in range(2):
        loads[("x", 2, a)].wait()
        pre_part(2, a)
        pre_send(2, a)
    hidden_of(1, 0)
    rw_add(2, rw_copy)
    rw_copy = rw_send(3)
    pre_chip(2, 0)
    pre_chip(2, 1)
    hidden_of(1, 1)
    loads["lg"].wait()
    rw_add(3, rw_copy)
    with scope("entering"):

        @pl.when(top)
        def _():
            sums = rw[4]
            means = sums[0:1, :] / jnp.maximum(sums[1:2, :], 1.0)
            position = lax.broadcasted_iota(jnp.int32, (ROWS, 128), 0)
            for n in range(2):
                begin = jnp.int32(0)
                weights = jnp.zeros((ROWS, 128), F32)
                for k in range(SEQS):
                    finish = begin + lengths[n, 0, k]
                    own = jnp.sum(
                        jnp.where(lane[0:1, :] == ids[n, 0, k], means, 0.0), axis=-1, keepdims=True
                    )
                    advantage = rewards[n, 0, k] - own
                    inside = jnp.logical_and(position >= begin, position < finish)
                    weights = weights + jnp.where(inside, advantage, 0.0)
                    begin = finish
                weight[n] = -weights

                def body(i, carry):
                    r = sixteen(i * 16)
                    values = weight[n, r, 0:1] * lg[n, r, :].astype(F32)
                    call[1, sixteen((n + 1) * ROWS + i * 16), :] = values.astype(BF16)
                    return carry

                lax.fori_loop(0, ROWS // 16, body, 0)

    shift_in(1, 0)
    back_part(1, 0)
    back_send(1, 0)
    hidden_of(2, 0)
    back_chip(1, 0)
    scaled_of(1, 0)
    gs_wait(1, 0)
    cot_out(1, 0)
    shift(1, 0)
    shift_in(1, 1)
    back_part(1, 1)
    back_send(1, 1)
    hidden_of(2, 1)
    back_chip(1, 1)
    scaled_of(1, 1)
    gs_wait(1, 1)
    cot_out(1, 1)
    shift(1, 1)
    for t in range(STEPS):
        for a in range(2):
            hid_copy[t, a].wait_recv()

    out0x, out0y = piece(0, gout, hid, call, 0)
    in0x, in0y = piece(1, gin, gs, gained, 0)
    out1x, out1y = piece(2, gout, hid, call, 1)
    in1x, in1y = piece(3, gin, gs, gained, 1)

    shift_in(2, 0)
    back_part(2, 0)
    back_send(2, 0)
    out0x.compute()
    out0x.h(0)
    out0x.f(0)
    back_chip(2, 0)
    out0y.compute()
    out0y.h(0)
    out0y.f(0)
    scaled_of(2, 0)
    shift_in(2, 1)
    back_part(2, 1)
    back_send(2, 1)
    out0x.m(0)
    gs_wait(2, 0)
    in0x.compute()
    in0x.h(0)
    out0y.m(0)
    back_chip(2, 1)
    in0y.compute()
    in0y.h(0)
    out1x.compute()
    in0x.f(0)
    out1x.h(0)
    out1y.compute()
    in0y.f(0)
    out1y.h(0)
    cot_out(2, 0)
    out0x.middle()
    out0y.middle()
    in0x.m(0)
    in0y.m(0)
    out1x.f(0)
    out1y.f(0)
    scaled_of(2, 1)
    gs_wait(2, 1)
    in1x.compute()
    in1x.h(0)
    in1y.compute()
    in1y.h(0)
    cot_out(2, 1)
    out1x.m(0)
    out1y.m(0)
    in1x.f(0)
    in1y.f(0)
    out0x.m(1)
    out0y.m(1)
    in0x.middle()
    in0y.middle()
    in1x.m(0)
    in1y.m(0)
    out0x.end()
    out0y.end()
    in0x.m(1)
    in0y.m(1)
    out1x.middle()
    out1y.middle()
    in0x.end()
    in0y.end()
    out1x.m(1)
    out1y.m(1)
    in1x.middle()
    in1y.middle()
    out1x.end()
    out1y.end()
    in1x.m(1)
    in1y.m(1)
    in1x.end()
    in1y.end()

    with scope("ends"):
        for sem, whole in classes.values():
            pltpu.make_async_remote_copy(
                src_ref=whole, dst_ref=whole, send_sem=sem, recv_sem=recv_sem.at[0],
                device_id=partner, device_id_type=MESH,
            ).wait_send()

        @pl.when(sec != 0)
        def _():
            shift_copy(0, 1).wait_send()
            shift_copy(1, 1).wait_send()

        shift_copy(0, 0).wait_send()
        shift_copy(1, 0).wait_send()
    assert recv_used[0] <= N_RECV and len(classes) <= N_SEND


def finish(gin, gout, leaving, gin_hbm, gout_hbm, leaving_hbm, sem):
    pairs = ((leaving, leaving_hbm), (gin, gin_hbm), (gout, gout_hbm))
    copies = [pltpu.make_async_copy(src, dst, sem.at[k]) for k, (src, dst) in enumerate(pairs)]
    for copy in copies:
        copy.start()
    for copy in copies:
        copy.wait()


def shards(saved, proj_in, proj_out, gain, arriving, logp, rewards, lengths, ids):
    sections = lax.axis_size("pipe")
    hbm = pl.BlockSpec(memory_space=pltpu.HBM)
    vmem = pl.BlockSpec(memory_space=pltpu.VMEM)
    V = pltpu.VMEM
    shapes = (
        jax.ShapeDtypeStruct((2, 32, DL), F32),
        jax.ShapeDtypeStruct((2, 32, DL), F32),
        jax.ShapeDtypeStruct((2, ROWS, DL), BF16),
    )
    results = pl.pallas_call(
        lambda *refs: kernel(sections, *refs),
        name="window",
        out_shape=shapes,
        in_specs=[hbm] * 9,
        out_specs=(vmem, vmem, vmem),
        scratch_shapes=[
            V((STEPS, 2, ROWS, DL), BF16),
            V((2, R, DL), BF16),
            V((2, R, DL), BF16),
            V((2, 1, DL), F32),
            V((2, ROWS, DL), BF16),
            V((2, STEPS * ROWS, DL), BF16),
            V((2, STEPS * ROWS, DL), BF16),
            V((2, STEPS * ROWS, R), BF16),
            V((2, STEPS * ROWS, R), BF16),
            V((STEPS, 2, ROWS, 128), F32),
            V((STEPS, 2, ROWS, R), BF16),
            V((STEPS, 2, ROWS, R), BF16),
            V((STEPS, 2, HALF, R), BF16),
            V((STEPS, 2, HALF, R), BF16),
            V((STEPS, 2, HALF, R), BF16),
            V((STEPS, 2, HALF, R), BF16),
            V((STEPS, 2, HALF, R), BF16),
            V((STEPS, 2, HALF, R), BF16),
            V((ROWS, 128), F32),
            V((STEPS, 2, 8, 128), F32),
            V((STEPS, 2, 8, 128), F32),
            V((STEPS, 2, 8, 128), F32),
            V((STEPS, 2, 8, 128), F32),
            V((STEPS, 2, HALF, 128), F32),
            V((STEPS, 2, HALF, R), F32),
            V((STEPS, 2, HALF, R), F32),
            V((STEPS - 1, 2, ROWS, DL), BF16),
            V((5, 8, 128), F32),
            V((4, 8, 128), F32),
            V((2, ROWS, 128), F32),
            pltpu.SMEM((2, 1, SEQS), F32),
            pltpu.SMEM((2, 1, SEQS), jnp.int32),
            pltpu.SMEM((2, 1, SEQS), jnp.int32),
            V((4, 4, 4, 32, DL), BF16),
            V((4, 2, 2, 32, DL), BF16),
            V((4, 2, 4, 32, DL), BF16),
            V((4, 4, 32, DL), BF16),
            V((4, 2, 16, DL), BF16),
            V((4, 2, 32, DL), BF16),
            pltpu.SemaphoreType.DMA((20,)),
            pltpu.SemaphoreType.DMA((N_SEND,)),
            pltpu.SemaphoreType.DMA((N_RECV,)),
            pltpu.SemaphoreType.DMA((4,)),
            pltpu.SemaphoreType.DMA((4,)),
        ],
        compiler_params=pltpu.CompilerParams(
            collective_id=0, has_side_effects=True, vmem_limit_bytes=40 * 2**20
        ),
    )(
        *(
            pltpu.with_memory_space_constraint(x, pltpu.HBM)
            for x in (
                saved[:, :, 0], proj_in[:, 0], proj_out[:, 0], gain, arriving[:, 0], logp,
                rewards, lengths, ids,
            )
        )
    )
    any_spec = pl.BlockSpec(memory_space=pl.ANY)
    results = pl.pallas_call(
        finish,
        name="finish",
        out_shape=shapes,
        in_specs=[vmem] * 3,
        out_specs=(any_spec,) * 3,
        scratch_shapes=[pltpu.SemaphoreType.DMA((3,))],
        compiler_params=pltpu.CompilerParams(vmem_limit_bytes=2**20),
    )(*results)
    return tuple(r[:, None] for r in results)


def solution(mesh):
    return jax.shard_map(
        shards,
        mesh=mesh,
        in_specs=(
            P(None, None, "pipe", "dp", "tensor"),
            P(None, "pipe", None, "tensor"),
            P(None, "pipe", None, "tensor"),
            P(None, "pipe", "tensor"),
            P(None, "pipe", "dp", "tensor"),
            P(None, "dp", "tensor"),
            P(None, "dp", None),
            P(None, "dp", None),
            P(None, "dp", None),
        ),
        out_specs=(
            P(None, "pipe", "dp", "tensor"),
            P(None, "pipe", "dp", "tensor"),
            P(None, "pipe", "dp", "tensor"),
        ),
        check_vma=False,
    )
```

time: 299 us -> 95.1 us (0.32)
  the two profiles are of different devices: /device:TPU:2 before, /device:TPU:8 now
where the time goes in v2:
time: 95.1 us; the launch traced here: 95 us
  Pallas kernels  94.4 us (99%)
    pallas_call x1, Pallas kernels, shards(): pl.pallas_call(lambda *refs: kernel(sections, *refs), name='window', out_...  93.4 us

profile of v2, /device:TPU:8, one launch (start us, length us, event | category | flops | bytes accessed | tf_op | source)
XLA Modules:
  0.0 95.0 jit_solution(1333296788548881030)
XLA Ops:
  0.6 93.4 %window.1 = (f32[2,32,1024]{2,1,0:T(8,128)S(1)}, f32[2,32,1024]{2,1,0:T(8,128)S(1)}, bf16[2,128,1024]{2,1,0:T(8,128)(2,1)S(1)}) custom-call(bf16[3,2,128,1024]{3,2,1,0:T(8,128)(2,1)} %bitcast.15, bf16[2,512,1024]{2,1,0:T(8,128)(2,1)} %bitcast.13, bf16[2,512,1024]{2,1,0:T(8,128)(2,1)} %bitcast.14, f32[2,1,1024]{2,1,0:T(1,128)} %refs_3_.1, ...), custom_call_target="tpu_custom_call" | custom-call | tf_op jit(solution)/shard_map/window/pallas_call | solution.py:640
  94.0 1.0 %finish.1 = (f32[2,32,1024]{2,1,0:T(8,128)}, f32[2,32,1024]{2,1,0:T(8,128)}, bf16[2,128,1024]{2,1,0:T(8,128)(2,1)}) custom-call(f32[2,32,1024]{2,1,0:T(8,128)S(1)} %get-tuple-element.9.gin, f32[2,32,1024]{2,1,0:T(8,128)S(1)} %get-tuple-element.10.gout, bf16[2,128,1024]{2,1,0:T(8,128)(2,1)S(1)} %get-tuple-element.11.leaving), custom_call_target="tpu_custom_call" | custom-call | tf_op jit(solution)/shard_map/finish/pallas_call | solution.py:705

commit v3 on v2

--- a/solution.py
+++ b/solution.py
@@ -17,9 +17,10 @@
 BF16 = jnp.bfloat16
 MESH = pl.DeviceIdType.MESH
 
-SPLITS = ((0, 768, "x"), (768, 256, "y"))
-N_RECV = 96
-N_SEND = 32
+IN_SPLIT = ((0, 1024, "x"),)
+OUT_SPLITS = (((0, 768, "x"), (768, 256, "y")), ((0, 768, "x"), (768, 256, "y")))
+N_RECV = 87
+N_SEND = 18
 scope = jax.named_scope
 
 
@@ -43,7 +44,7 @@
     part_pre, part_back, d_pre, d_back, chip_pre, chip_back, y_pre, y_back,
     sqp, sq, sq_d, sq_chip, sq_y, inv, slope, presum, cout,
     rw, rw_in, weight, rewards, lengths, ids,
-    g, h1, f1, s1, h2, f2,
+    g, h1, f1, s1, h2, f2, gx, gl,
     load_sem, send_sem, recv_sem, shift_send, shift_recv,
 ):
     sec = lax.axis_index("pipe")
@@ -56,8 +57,7 @@
     other = pl.multiple_of((1 - core) * HALF, HALF)
     top = sec == sections - 1
     early = [jnp.where(sec == 0, 1 - a, a) for a in range(2)]
-    late = [jnp.where(top, 1 - a, a) for a in range(2)]
-    block = [early, early, late]
+    block = [early, [0, 1], [0, 1]]
 
     partner = (sec, dp, tn + 1 - 2 * core)
     across = (sec, dp, (tn + 2) % 4)
@@ -74,7 +74,8 @@
         return (i + by) % 4
 
     peers = [partner, across, below, above]
-    peers += [at_x(ring(xi, 1)), at_x(ring(xi, 3)), at_y(ring(yi, 1)), at_y(ring(yi, 3))]
+    peers += [at_x(ring(xi, by)) for by in (1, 2, 3)]
+    peers += [at_y(ring(yi, by)) for by in (1, 2, 3)]
     barrier = pltpu.get_barrier_semaphore()
     for peer in peers:
         pl.semaphore_signal(barrier, inc=1, device_id=peer, device_id_type=MESH)
@@ -120,12 +121,12 @@
         load(("win", a), win_hbm.at[v], win.at[v])
         load(("c", a), arriving_hbm.at[v], call.at[v, pl.ds(0, ROWS)])
         load(("wout", a), wout_hbm.at[v], wout.at[v])
-    for t in (1, 2):
-        for a in range(2):
-            load(("x", t, a), saved_hbm.at[t, block[t][a]], xs.at[t, block[t][a]])
-    load("rewards", rewards_hbm, rewards)
-    load("lengths", lengths_hbm, lengths)
-    load("ids", ids_hbm, ids)
+        if a == 0:
+            load("rewards", rewards_hbm, rewards)
+            load("lengths", lengths_hbm, lengths)
+            load("ids", ids_hbm, ids)
+    for t in (2, 1):
+        load(("x", t), saved_hbm.at[t], xs.at[t])
     load("lg", logp_hbm, lg)
 
     rows_of = [pl.ds(t * ROWS, ROWS) for t in range(STEPS)]
@@ -283,19 +284,23 @@
                     leaving[v, :, cols] = out
 
     def shift_copy(t, a):
+        slot = a if t == 0 or a == 0 else jnp.where(sec == 0, 0, 1)
         return pltpu.make_async_remote_copy(
-            src_ref=cout.at[t, a], dst_ref=call.at[a, rows_of[t + 1]],
-            send_sem=shift_send.at[t * 2 + a], recv_sem=shift_recv.at[t * 2 + a],
+            src_ref=cout.at[t, a], dst_ref=call.at[slot, rows_of[t + 1]],
+            send_sem=shift_send.at[t * 2 + a], recv_sem=shift_recv.at[t * 2 + slot],
             device_id=below, device_id_type=MESH,
         )
 
-    def shift(t, a):
-        if a == 0:
-            shift_copy(t, a).start()
+    def shift_do(t, a, what):
+        if a == t:
+            what(shift_copy(t, a))
         else:
             @pl.when(sec != 0)
             def _():
-                shift_copy(t, a).start()
+                what(shift_copy(t, a))
+
+    def shift(t, a):
+        shift_do(t, a, lambda copy: copy.start())
 
     def shift_in(t, a):
         v = block[t][a]
@@ -306,7 +311,8 @@
                 arrived(call.at[v, rows_of[t]], shift_recv.at[(t - 1) * 2 + v])
 
     class Ring:
-        def __init__(self, p, out, v, first, width, axis):
+        def __init__(self, p, out, v, direct, first, width, axis):
+            self.direct = direct
             self.p, self.out, self.v = p, out, v
             self.first, self.width = first, width
             self.name = f"{p}{axis}"
@@ -322,8 +328,8 @@
             self.chunk = (chunk, small)
             self.n = (2, 16)
             self.half = (h1.at[p, :, :, :, cols], h2.at[p, :, :, cols])
-            self.full = (f1.at[p, :, :, :, cols], f2.at[p, :, :, cols])
-            self.half_recv = [recv_slot() for _ in range(2)]
+            self.full = (f1.at[p, :, :, :, cols], f2.at[p, pl.ds(0, 3 if direct else 2), :, cols])
+            self.half_recv = [recv_slot() for _ in range(1 if direct else 2)]
             self.full_recv = [recv_slot() for _ in range(2)]
 
         def go(self, phase, j, lo, d, full):
@@ -333,10 +339,12 @@
             to = at(ring(i, (1, 3)[d]))
             if full:
                 dst = self.full[phase].at[d, pl.ds(lo, n)]
-                remote(src, dst, to, f"f{phase}", (f1, f2)[phase], self.full_recv[phase])
+                whole = (f1, f2.at[pl.ds(0, 2), pl.ds(0, 2)])[phase]
+                remote(src, dst, to, f"f{phase}", whole, self.full_recv[phase])
             else:
                 dst = self.half[phase].at[d]
-                remote(src, dst, to, f"h{phase}", (h1, h2)[phase], self.half_recv[phase])
+                whole = (h1, h2.at[pl.ds(0, 2)])[phase]
+                remote(src, dst, to, f"h{phase}", whole, self.half_recv[phase])
 
         def h(self, phase):
             far, n = ring(self.axes[phase][0], 2), self.n[phase]
@@ -358,6 +366,19 @@
                     chunk[...] = (chunk[...].astype(F32) + came[...].astype(F32)).astype(BF16)
                     self.go(phase, j, lo, d, True)
 
+        def second(self):
+            if not self.direct:
+                self.h(1)
+                self.f(1)
+                return
+            i, at = self.axes[1]
+            for k, by in enumerate((2, 1, 3)):
+                j = ring(i, by)
+                remote(
+                    self.chunk[1](j, 0, 32), self.full[1].at[k], at(j), "direct",
+                    f2.at[pl.ds(0, 2)], self.full_recv[1],
+                )
+
         def middle(self):
             with scope(f"mid_{self.name}"):
                 arrived(self.full[0], self.full_recv[0])
@@ -367,56 +388,75 @@
                     for d in range(2):
                         total = total + f1[self.p, d, k, :, self.cols].astype(F32)
                     s1[self.p, k, :, self.cols] = total.astype(BF16)
-                self.h(1)
-                self.f(1)
+                self.second()
 
         def end(self):
             with scope(f"end_{self.name}"):
                 arrived(self.full[1], self.full_recv[1])
                 total = s1[self.p, self.axes[1][0], :, self.cols].astype(F32)
-                for d in range(2):
+                for d in range(3 if self.direct else 2):
                     total = total + f2[self.p, d, :, self.cols].astype(F32)
                 self.out[self.v, :, self.cols] = total * (1.0 / (16 * ROWS))
 
-    def piece(p, out, left, right, a):
-        v = block[2][a]
-        rings = [Ring(p, out, v, *split) for split in SPLITS]
-
-        def compute(ring_):
-            with scope(f"grad_{ring_.name}"):
-                lhs = left[v]
-                for k in range(ring_.width // 256):
-                    cols = pl.ds(ring_.first + k * 256, 256)
-                    made = dot_tn(lhs, right[v, :, cols]).astype(BF16)
-                    g[p, :, :, :, cols] = made.reshape(4, 4, 32, 256)
-
-        for ring_ in rings:
-            ring_.compute = lambda ring_=ring_: compute(ring_)
-        return rings
+    def grad(p, left, right, v, steps):
+        with scope(f"grad_{p}"):
+            tokens = pl.ds(0, steps * ROWS)
+            lhs = left[v, tokens, :]
+            for k in (3, 0, 1, 2):
+                cols = pl.ds(k * 256, 256)
+                made = dot_tn(lhs, right[v, tokens, cols]).astype(BF16)
+                g[p, :, :, :, cols] = made.reshape(4, 4, 32, 256)
+
+    gx_recv = [[recv_slot() for _ in range(3)] for _ in range(2)]
+    gl_recv = [recv_slot() for _ in range(2)]
+    nxt, prv, far = (at_x(ring(xi, by)) for by in (1, 3, 2))
+
+    def slot_rows(k, lo=0, n=ROWS):
+        return pl.ds(k * ROWS + lo, n)
+
+    def gather(v):
+        own = gained.at[v, rows_of[2]]
+        remote(own, gx.at[v, slot_rows(0)], nxt, "gx", gx.at[:, pl.ds(0, 2 * ROWS)], gx_recv[v][0])
+        remote(own, gx.at[v, slot_rows(1)], prv, "gx", None, gx_recv[v][1])
+
+    def forward(v):
+        with scope(f"forward{v}"):
+            for k, lo, to in ((0, 0, nxt), (1, HALF, prv)):
+                arrived(gx.at[v, slot_rows(k)], gx_recv[v][k])
+                remote(
+                    gx.at[v, slot_rows(k, lo, HALF)], gx.at[v, slot_rows(2, lo, HALF)], to, "gx2",
+                    gx.at[:, pl.ds(0, ROWS)], gx_recv[v][2],
+                )
+
+    def left_send(v):
+        for k, by, to in ((0, 1, nxt), (1, 3, prv), (2, 2, far)):
+            cols = pl.ds(pl.multiple_of(ring(xi, by) * 128, 128), 128)
+            remote(gs.at[v, rows_of[2], cols], gl.at[v, slot_rows(k)], to, "gl", gl, gl_recv[v])
+
+    def in_middle(ring_):
+        v, p = ring_.v, ring_.p
+        with scope(f"mid_{ring_.name}"):
+            arrived(ring_.full[0], ring_.full_recv[0])
+            arrived(gx.at[v, slot_rows(2)], gx_recv[v][2])
+            arrived(gl.at[v], gl_recv[v])
+            own = gs[v, rows_of[2], pl.ds(pl.multiple_of(xi * 128, 128), 128)]
+            for k in range(4):
+                cols = pl.ds(k * 256, 256)
+                total = dot_tn(gl[v], gx[v, :, cols]) + dot_tn(own, gained[v, rows_of[2], cols])
+                total = total + g[p, xi, :, :, cols].reshape(128, 256).astype(F32)
+                for d in range(2):
+                    total = total + f1[p, d, :, :, cols].reshape(128, 256).astype(F32)
+                s1[p, :, :, cols] = total.astype(BF16).reshape(4, 32, 256)
+            ring_.second()
 
     loads["gain"].wait()
-    loads[("x", 0, 0)].wait()
-    loads[("win", 0)].wait()
-    pre_part(0, 0)
-    loads[("c", 0)].wait()
-    loads[("wout", 0)].wait()
-    back_part(0, 0)
-    with scope("barrier"):
-        pl.semaphore_wait(barrier, len(peers))
-    pre_send(0, 0)
-    back_send(0, 0)
-    loads[("x", 0, 1)].wait()
-    loads[("win", 1)].wait()
-    pre_part(0, 1)
-    pre_send(0, 1)
-    pre_chip(0, 0)
-    back_chip(0, 0)
-    loads[("c", 1)].wait()
-    loads[("wout", 1)].wait()
-    back_part(0, 1)
-    back_send(0, 1)
-    pre_chip(0, 1)
-
+    for a in range(2):
+        loads[("x", 0, a)].wait()
+        loads[("win", a)].wait()
+        pre_part(0, a)
+        loads[("c", a)].wait()
+        loads[("wout", a)].wait()
+        back_part(0, a)
     for name in ("rewards", "lengths", "ids"):
         loads[name].wait()
     lane = lax.broadcasted_iota(jnp.int32, (8, 128), 1)
@@ -428,57 +468,78 @@
             amount = jnp.where(line == 0, rewards[n, 0, k], jnp.where(line == 1, 1.0, 0.0))
             tile = tile + jnp.where(member, amount, 0.0)
     rw[0] = tile
-    partners = [at_x(xi + 1 - 2 * (xi % 2)), at_x(3 - xi), at_y(yi + 1 - 2 * (yi % 2)), at_y(3 - yi)]
+    with scope("barrier"):
+        pl.semaphore_wait(barrier, len(peers))
+    for a in range(2):
+        pre_send(0, a)
+        back_send(0, a)
+    rw_x = [
+        remote(rw.at[0], rw_in.at[k], to, "rw", rw_in) for k, to in ((0, nxt), (1, prv), (2, far))
+    ]
+    rw_y = [at_y(yi + 1 - 2 * (yi % 2)), at_y(3 - yi)]
 
     def rw_send(k):
-        return remote(rw.at[k], rw_in.at[k], partners[k], "rw", rw_in)
+        return remote(rw.at[k], rw_in.at[k + 2], rw_y[k - 1], "rw", rw_in)
 
     def rw_add(k, copy):
-        copy.wait_recv()
-        rw[k + 1] = rw[k] + rw_in[k]
-
-    rw_copy = rw_send(0)
-    back_chip(0, 1)
-    loads[("x", 1, 0)].wait()
+        with scope(f"rw{k}"):
+            copy.wait_recv()
+            rw[k + 1] = rw[k] + rw_in[k + 2]
+
+    loads[("x", 2)].wait()
+    pre_part(2, 0)
+    gather(0)
+    pre_chip(0, 0)
+    back_chip(0, 0)
+    pre_send(2, 0)
+    pre_part(2, 1)
+    gather(1)
+    pre_send(2, 1)
+    loads[("x", 1)].wait()
     pre_part(1, 0)
     pre_send(1, 0)
+    pre_chip(0, 1)
+    back_chip(0, 1)
+    pre_part(1, 1)
+    pre_send(1, 1)
     hidden_of(0, 0)
     scaled_of(0, 0)
-    pre_chip(1, 0)
+    with scope("rwx"):
+        for copy in rw_x:
+            copy.wait_recv()
+        rw[1] = rw[0] + rw_in[0] + rw_in[1] + rw_in[2]
+    rw_copy = rw_send(1)
     gs_wait(0, 0)
     cot_out(0, 0)
     shift(0, 0)
-    rw_add(0, rw_copy)
-    rw_copy = rw_send(1)
-    loads[("x", 1, 1)].wait()
-    pre_part(1, 1)
-    pre_send(1, 1)
     hidden_of(0, 1)
+    pre_chip(1, 0)
     scaled_of(0, 1)
-    pre_chip(1, 1)
     gs_wait(0, 1)
     cot_out(0, 1)
     shift(0, 1)
 
     rw_add(1, rw_copy)
     rw_copy = rw_send(2)
-    for a in range(2):
-        loads[("x", 2, a)].wait()
-        pre_part(2, a)
-        pre_send(2, a)
-    hidden_of(1, 0)
-    rw_add(2, rw_copy)
-    rw_copy = rw_send(3)
+    pre_chip(1, 1)
     pre_chip(2, 0)
     pre_chip(2, 1)
+    forward(0)
+    hidden_of(1, 0)
+
+    shift_in(1, 0)
+    back_part(1, 0)
+    back_send(1, 0)
     hidden_of(1, 1)
+    back_chip(1, 0)
+    forward(1)
+    rw_add(2, rw_copy)
     loads["lg"].wait()
-    rw_add(3, rw_copy)
     with scope("entering"):
 
         @pl.when(top)
         def _():
-            sums = rw[4]
+            sums = rw[3]
             means = sums[0:1, :] / jnp.maximum(sums[1:2, :], 1.0)
             position = lax.broadcasted_iota(jnp.int32, (ROWS, 128), 0)
             for n in range(2):
@@ -503,103 +564,80 @@
 
                 lax.fori_loop(0, ROWS // 16, body, 0)
 
-    shift_in(1, 0)
-    back_part(1, 0)
-    back_send(1, 0)
     hidden_of(2, 0)
-    back_chip(1, 0)
     scaled_of(1, 0)
+    shift_in(1, 1)
+    back_part(1, 1)
+    back_send(1, 1)
     gs_wait(1, 0)
     cot_out(1, 0)
     shift(1, 0)
-    shift_in(1, 1)
-    back_part(1, 1)
-    back_send(1, 1)
+
+    out0x, out0y = (Ring(0, gout, 0, True, *split) for split in OUT_SPLITS[0])
+    out1x, out1y = (Ring(2, gout, 1, True, *split) for split in OUT_SPLITS[1])
+    in0, in1 = (Ring(1 + 2 * v, gin, v, False, *IN_SPLIT[0]) for v in range(2))
     hidden_of(2, 1)
     back_chip(1, 1)
+    grad(1, gs, gained, 0, 2)
+    in0.h(0)
+    in0.f(0)
+    for t in range(STEPS):
+        for a in range(2):
+            hid_copy[t, a].wait_recv()
     scaled_of(1, 1)
     gs_wait(1, 1)
     cot_out(1, 1)
     shift(1, 1)
-    for t in range(STEPS):
-        for a in range(2):
-            hid_copy[t, a].wait_recv()
-
-    out0x, out0y = piece(0, gout, hid, call, 0)
-    in0x, in0y = piece(1, gin, gs, gained, 0)
-    out1x, out1y = piece(2, gout, hid, call, 1)
-    in1x, in1y = piece(3, gin, gs, gained, 1)
+    grad(3, gs, gained, 1, 2)
+    in1.h(0)
 
     shift_in(2, 0)
     back_part(2, 0)
     back_send(2, 0)
-    out0x.compute()
+    in0.m(0)
+    grad(0, hid, call, 0, 3)
+    back_chip(2, 0)
     out0x.h(0)
     out0x.f(0)
-    back_chip(2, 0)
-    out0y.compute()
+    scaled_of(2, 0)
+    gs_wait(2, 0)
+    left_send(0)
     out0y.h(0)
-    out0y.f(0)
-    scaled_of(2, 0)
     shift_in(2, 1)
     back_part(2, 1)
     back_send(2, 1)
+    grad(2, hid, call, 1, 3)
+    back_chip(2, 1)
     out0x.m(0)
-    gs_wait(2, 0)
-    in0x.compute()
-    in0x.h(0)
+    in1.m(0)
+    in1.f(0)
+    cot_out(2, 0)
     out0y.m(0)
-    back_chip(2, 1)
-    in0y.compute()
-    in0y.h(0)
-    out1x.compute()
-    in0x.f(0)
-    out1x.h(0)
-    out1y.compute()
-    in0y.f(0)
-    out1y.h(0)
-    cot_out(2, 0)
-    out0x.middle()
-    out0y.middle()
-    in0x.m(0)
-    in0y.m(0)
-    out1x.f(0)
-    out1y.f(0)
+    out0y.f(0)
+    in_middle(in0)
     scaled_of(2, 1)
     gs_wait(2, 1)
-    in1x.compute()
-    in1x.h(0)
-    in1y.compute()
-    in1y.h(0)
+    left_send(1)
+    out1x.h(0)
+    out1y.h(0)
+    out0x.middle()
     cot_out(2, 1)
+    out1x.f(0)
+    out0y.middle()
+    in0.m(1)
     out1x.m(0)
     out1y.m(0)
-    in1x.f(0)
-    in1y.f(0)
-    out0x.m(1)
-    out0y.m(1)
-    in0x.middle()
-    in0y.middle()
-    in1x.m(0)
-    in1y.m(0)
+    out1y.f(0)
+    in_middle(in1)
     out0x.end()
+    in0.end()
     out0y.end()
-    in0x.m(1)
-    in0y.m(1)
+    out1y.middle()
     out1x.middle()
-    out1y.middle()
-    in0x.end()
-    in0y.end()
-    out1x.m(1)
-    out1y.m(1)
-    in1x.middle()
-    in1y.middle()
+    in1.m(1)
+    in1.end()
+    out1y.end()
     out1x.end()
-    out1y.end()
-    in1x.m(1)
-    in1y.m(1)
-    in1x.end()
-    in1y.end()
 
     with scope("ends"):
         for sem, whole in classes.values():
@@ -608,14 +646,10 @@
                 device_id=partner, device_id_type=MESH,
             ).wait_send()
 
-        @pl.when(sec != 0)
-        def _():
-            shift_copy(0, 1).wait_send()
-            shift_copy(1, 1).wait_send()
-
-        shift_copy(0, 0).wait_send()
-        shift_copy(1, 0).wait_send()
-    assert recv_used[0] <= N_RECV and len(classes) <= N_SEND
+        for t in range(STEPS - 1):
+            for a in range(2):
+                shift_do(t, a, lambda copy: copy.wait_send())
+    assert (recv_used[0], len(classes), len(loads)) == (N_RECV, N_SEND, 15), (recv_used[0], len(classes), len(loads))
 
 
 def finish(gin, gout, leaving, gin_hbm, gout_hbm, leaving_hbm, sem):
@@ -671,8 +705,8 @@
             V((STEPS, 2, HALF, R), F32),
             V((STEPS, 2, HALF, R), F32),
             V((STEPS - 1, 2, ROWS, DL), BF16),
+            V((4, 8, 128), F32),
             V((5, 8, 128), F32),
-            V((4, 8, 128), F32),
             V((2, ROWS, 128), F32),
             pltpu.SMEM((2, 1, SEQS), F32),
             pltpu.SMEM((2, 1, SEQS), jnp.int32),
@@ -682,8 +716,10 @@
             V((4, 2, 4, 32, DL), BF16),
             V((4, 4, 32, DL), BF16),
             V((4, 2, 16, DL), BF16),
-            V((4, 2, 32, DL), BF16),
-            pltpu.SemaphoreType.DMA((20,)),
+            V((4, 3, 32, DL), BF16),
+            V((2, 3 * ROWS, DL), BF16),
+            V((2, 3 * ROWS, 128), BF16),
+            pltpu.SemaphoreType.DMA((15,)),
             pltpu.SemaphoreType.DMA((N_SEND,)),
             pltpu.SemaphoreType.DMA((N_RECV,)),
             pltpu.SemaphoreType.DMA((4,)),

time: 95.1 us -> 85.6 us (0.900)
  Pallas kernels: 94.4 us -> 84.8 us
    pallas_call x1, Pallas kernels: 93.4 us -> 83.8 us  [shards(): pl.pallas_call(lambda *refs: kernel(sections, *refs), name='window', out_...]
where the time goes in v3:
time: 85.6 us; the launch traced here: 85.4 us
  Pallas kernels  84.8 us (99%)
    pallas_call x1, Pallas kernels, shards(): pl.pallas_call(lambda *refs: kernel(sections, *refs), name='window', out_...  83.8 us

profile of v3, /device:TPU:8, one launch (start us, length us, event | category | flops | bytes accessed | tf_op | source)
XLA Modules:
  0.0 85.4 jit_solution(12665479640069360048)
XLA Ops:
  0.6 83.8 %window.1 = (f32[2,32,1024]{2,1,0:T(8,128)S(1)}, f32[2,32,1024]{2,1,0:T(8,128)S(1)}, bf16[2,128,1024]{2,1,0:T(8,128)(2,1)S(1)}) custom-call(bf16[3,2,128,1024]{3,2,1,0:T(8,128)(2,1)} %bitcast.15, bf16[2,512,1024]{2,1,0:T(8,128)(2,1)} %bitcast.13, bf16[2,512,1024]{2,1,0:T(8,128)(2,1)} %bitcast.14, f32[2,1,1024]{2,1,0:T(1,128)} %refs_3_.1, ...), custom_call_target="tpu_custom_call" | custom-call | tf_op jit(solution)/shard_map/window/pallas_call | solution.py:674
  84.4 1.0 %finish.1 = (f32[2,32,1024]{2,1,0:T(8,128)}, f32[2,32,1024]{2,1,0:T(8,128)}, bf16[2,128,1024]{2,1,0:T(8,128)(2,1)}) custom-call(f32[2,32,1024]{2,1,0:T(8,128)S(1)} %get-tuple-element.9.gin, f32[2,32,1024]{2,1,0:T(8,128)S(1)} %get-tuple-element.10.gout, bf16[2,128,1024]{2,1,0:T(8,128)(2,1)S(1)} %get-tuple-element.11.leaving), custom_call_target="tpu_custom_call" | custom-call | tf_op jit(solution)/shard_map/finish/pallas_call | solution.py:741

commit v4 on v3

--- a/solution.py
+++ b/solution.py
@@ -18,8 +18,11 @@
 MESH = pl.DeviceIdType.MESH
 
 IN_SPLIT = ((0, 1024, "x"),)
-OUT_SPLITS = (((0, 768, "x"), (768, 256, "y")), ((0, 768, "x"), (768, 256, "y")))
-N_RECV = 87
+OUT_SPLITS = (
+    ((0, 768, "x"), (768, 256, "y")),
+    ((0, 384, "x"), (384, 384, "x"), (768, 256, "y")),
+)
+N_RECV = 90
 N_SEND = 18
 scope = jax.named_scope
 
@@ -114,20 +117,24 @@
         copy.start()
         loads[name] = copy
 
-    load("gain", gain_hbm, gain)
-    for a in range(2):
+    def load_block(a):
         v = early[a]
         load(("x", 0, a), saved_hbm.at[0, v], xs.at[0, v])
         load(("win", a), win_hbm.at[v], win.at[v])
         load(("c", a), arriving_hbm.at[v], call.at[v, pl.ds(0, ROWS)])
         load(("wout", a), wout_hbm.at[v], wout.at[v])
-        if a == 0:
-            load("rewards", rewards_hbm, rewards)
-            load("lengths", lengths_hbm, lengths)
-            load("ids", ids_hbm, ids)
-    for t in (2, 1):
-        load(("x", t), saved_hbm.at[t], xs.at[t])
-    load("lg", logp_hbm, lg)
+
+    load("gain", gain_hbm, gain)
+    load_block(0)
+
+    def load_rest():
+        load_block(1)
+        load("rewards", rewards_hbm, rewards)
+        load("lengths", lengths_hbm, lengths)
+        load("ids", ids_hbm, ids)
+        for t in (2, 1):
+            load(("x", t), saved_hbm.at[t], xs.at[t])
+        load("lg", logp_hbm, lg)
 
     rows_of = [pl.ds(t * ROWS, ROWS) for t in range(STEPS)]
 
@@ -315,7 +322,7 @@
             self.direct = direct
             self.p, self.out, self.v = p, out, v
             self.first, self.width = first, width
-            self.name = f"{p}{axis}"
+            self.name = f"{p}{axis}{first}"
             cols = self.cols = pl.ds(first, width)
             pair = ((xi, at_x), (yi, at_y))
             if axis == "x":
@@ -450,13 +457,27 @@
             ring_.second()
 
     loads["gain"].wait()
-    for a in range(2):
-        loads[("x", 0, a)].wait()
-        loads[("win", a)].wait()
-        pre_part(0, a)
-        loads[("c", a)].wait()
-        loads[("wout", a)].wait()
-        back_part(0, a)
+    loads[("x", 0, 0)].wait()
+    loads[("win", 0)].wait()
+    load_rest()
+    pre_part(0, 0)
+    loads[("c", 0)].wait()
+    loads[("wout", 0)].wait()
+    back_part(0, 0)
+    with scope("barrier"):
+        pl.semaphore_wait(barrier, len(peers))
+    pre_send(0, 0)
+    back_send(0, 0)
+    loads[("x", 0, 1)].wait()
+    loads[("win", 1)].wait()
+    pre_part(0, 1)
+    pre_send(0, 1)
+    loads[("c", 1)].wait()
+    loads[("wout", 1)].wait()
+    back_part(0, 1)
+    back_send(0, 1)
+    pre_chip(0, 0)
+    back_chip(0, 0)
     for name in ("rewards", "lengths", "ids"):
         loads[name].wait()
     lane = lax.broadcasted_iota(jnp.int32, (8, 128), 1)
@@ -468,11 +489,6 @@
             amount = jnp.where(line == 0, rewards[n, 0, k], jnp.where(line == 1, 1.0, 0.0))
             tile = tile + jnp.where(member, amount, 0.0)
     rw[0] = tile
-    with scope("barrier"):
-        pl.semaphore_wait(barrier, len(peers))
-    for a in range(2):
-        pre_send(0, a)
-        back_send(0, a)
     rw_x = [
         remote(rw.at[0], rw_in.at[k], to, "rw", rw_in) for k, to in ((0, nxt), (1, prv), (2, far))
     ]
@@ -489,19 +505,16 @@
     loads[("x", 2)].wait()
     pre_part(2, 0)
     gather(0)
-    pre_chip(0, 0)
-    back_chip(0, 0)
     pre_send(2, 0)
+    pre_chip(0, 1)
+    back_chip(0, 1)
     pre_part(2, 1)
     gather(1)
     pre_send(2, 1)
     loads[("x", 1)].wait()
-    pre_part(1, 0)
-    pre_send(1, 0)
-    pre_chip(0, 1)
-    back_chip(0, 1)
-    pre_part(1, 1)
-    pre_send(1, 1)
+    for a in range(2):
+        pre_part(1, a)
+        pre_send(1, a)
     hidden_of(0, 0)
     scaled_of(0, 0)
     with scope("rwx"):
@@ -574,7 +587,7 @@
     shift(1, 0)
 
     out0x, out0y = (Ring(0, gout, 0, True, *split) for split in OUT_SPLITS[0])
-    out1x, out1y = (Ring(2, gout, 1, True, *split) for split in OUT_SPLITS[1])
+    out1a, out1b, out1y = (Ring(2, gout, 1, True, *split) for split in OUT_SPLITS[1])
     in0, in1 = (Ring(1 + 2 * v, gin, v, False, *IN_SPLIT[0]) for v in range(2))
     hidden_of(2, 1)
     back_chip(1, 1)
@@ -608,36 +621,41 @@
     back_send(2, 1)
     grad(2, hid, call, 1, 3)
     back_chip(2, 1)
+    out1a.h(0)
+    out1b.h(0)
     out0x.m(0)
-    in1.m(0)
-    in1.f(0)
     cot_out(2, 0)
     out0y.m(0)
     out0y.f(0)
+    in1.m(0)
+    in1.f(0)
     in_middle(in0)
     scaled_of(2, 1)
     gs_wait(2, 1)
     left_send(1)
-    out1x.h(0)
     out1y.h(0)
+    out1a.m(0)
+    out1b.m(0)
+    out1a.f(0)
+    out1b.f(0)
     out0x.middle()
+    out0y.middle()
     cot_out(2, 1)
-    out1x.f(0)
-    out0y.middle()
     in0.m(1)
-    out1x.m(0)
     out1y.m(0)
     out1y.f(0)
     in_middle(in1)
+    out1a.middle()
+    out1b.middle()
     out0x.end()
     in0.end()
     out0y.end()
     out1y.middle()
-    out1x.middle()
     in1.m(1)
     in1.end()
     out1y.end()
-    out1x.end()
+    out1a.end()
+    out1b.end()
 
     with scope("ends"):
         for sem, whole in classes.values():

time: 85.6 us -> 85.4 us (level)
  no operation moved by 1% of the time
where the time goes in v4:
time: 85.4 us; the launch traced here: 84.9 us
  Pallas kernels  84.3 us (99%)
    pallas_call x1, Pallas kernels, shards(): pl.pallas_call(lambda *refs: kernel(sections, *refs), name='window', out_...  83.3 us

profile of v4, /device:TPU:8, one launch (start us, length us, event | category | flops | bytes accessed | tf_op | source)
XLA Modules:
  0.0 84.9 jit_solution(4343326071458792447)
XLA Ops:
  0.6 83.3 %window.1 = (f32[2,32,1024]{2,1,0:T(8,128)S(1)}, f32[2,32,1024]{2,1,0:T(8,128)S(1)}, bf16[2,128,1024]{2,1,0:T(8,128)(2,1)S(1)}) custom-call(bf16[3,2,128,1024]{3,2,1,0:T(8,128)(2,1)} %bitcast.15, bf16[2,512,1024]{2,1,0:T(8,128)(2,1)} %bitcast.13, bf16[2,512,1024]{2,1,0:T(8,128)(2,1)} %bitcast.14, f32[2,1,1024]{2,1,0:T(1,128)} %refs_3_.1, ...), custom_call_target="tpu_custom_call" | custom-call | tf_op jit(solution)/shard_map/window/pallas_call | solution.py:692
  83.9 1.0 %finish.1 = (f32[2,32,1024]{2,1,0:T(8,128)}, f32[2,32,1024]{2,1,0:T(8,128)}, bf16[2,128,1024]{2,1,0:T(8,128)(2,1)}) custom-call(f32[2,32,1024]{2,1,0:T(8,128)S(1)} %get-tuple-element.9.gin, f32[2,32,1024]{2,1,0:T(8,128)S(1)} %get-tuple-element.10.gout, bf16[2,128,1024]{2,1,0:T(8,128)(2,1)S(1)} %get-tuple-element.11.leaving), custom_call_target="tpu_custom_call" | custom-call | tf_op jit(solution)/shard_map/finish/pallas_call | solution.py:759
